TPU v7x, 32 devices: a whole 2x2x4 slice. The times are simulated.
32 devices in a mesh: pipe: 2 (over x), tensor: 4 (over y, core), dp: 4 (over z).
Axes of the slice: x: 2, y: 2, z: 4, core: 2. Of those that a mesh axis runs over, the one named last changes fastest.
Arguments:
- inputs: bfloat16 [2, 512, 16384], P(None, 'dp', 'tensor'), may hold values from -6 to 6
- w_in: bfloat16 [2, 16384, 1024], P('pipe', ('tensor', 'dp')), may hold values from -0.046875 to 0.046875
- w_out: bfloat16 [2, 1024, 16384], P('pipe', None, ('tensor', 'dp')), may hold values from -0.1875 to 0.1875
- cotangent: bfloat16 [2, 512, 16384], P(None, 'dp', 'tensor'), may hold values from -6 to 6
Outputs:
- update_in: float32 [2, 16384, 1024], P('pipe', ('tensor', 'dp'))
- update_out: float32 [2, 1024, 16384], P('pipe', None, ('tensor', 'dp'))
- grad_norm: float32 [], replicated
All inputs are finite; a program needn't handle non-finite values.
Results may differ from a plain program's by a relative error of at most 0.008.
Values may be sent and summed in bfloat16 or wider, within the bound.
A program may use at most 192 MiB of HBM per device.

v0:
```python
import jax
import jax.numpy as jnp
from jax import lax
from jax.sharding import PartitionSpec as P

CLIP_NORM = 16384


def from_behind(value, axis, by):
    count = lax.axis_size(axis)
    pairs = [(i, i + by) for i in range(count) if 0 <= i + by < count]
    return lax.ppermute(value, axis, pairs)


def unit_forward(preact, unused):
    return jax.nn.silu(preact).astype(jnp.bfloat16)


def unit_backward(upward, preact):
    sigmoid_value = jax.nn.sigmoid(preact)
    return (upward * sigmoid_value * (1.0 + preact * (1.0 - sigmoid_value))).astype(jnp.bfloat16)


def kahan_add(running, carried, grad_term):
    corrected = grad_term - carried.astype(jnp.float32)
    summed = (running.astype(jnp.float32) + corrected).astype(jnp.bfloat16)
    carried = (summed.astype(jnp.float32) - running.astype(jnp.float32) - corrected).astype(
        jnp.bfloat16
    )
    return (summed, carried)


def contract_last(first_operand, second_operand):
    return lax.dot_general(
        first_operand, second_operand, (((1,), (1,)), ((), ())), preferred_element_type=jnp.float32
    )


def keep_state(state, x_part, act_part, err_part, slope_part):
    return state


def on_device(inputs, w_in, w_out, cotangent):
    sections = lax.axis_size("pipe")
    section_index = lax.axis_index("pipe")
    micro_count = inputs.shape[0]
    step_count = micro_count + sections - 1
    w_first, w_second = (w_in[0], w_out[0])
    section_inputs, section_seeds = (
        lax.all_to_all(inputs, "dp", split_axis=2, concat_axis=1, tiled=True),
        lax.all_to_all(cotangent, "dp", split_axis=2, concat_axis=1, tiled=True),
    )
    groups = lax.axis_size("dp")
    stat_rows = section_inputs.shape[1] // (lax.axis_size("tensor") * lax.axis_size("dp"))

    def combine_units(partial_value, unit_fn, kept_stat):
        share_part = lax.psum_scatter(
            partial_value, ("tensor", "dp"), scatter_dimension=0, tiled=True
        )
        return (
            share_part,
            lax.all_gather(unit_fn(share_part, kept_stat), ("tensor", "dp"), axis=0, tiled=True),
        )

    row_count = section_inputs.shape[1]
    col_count = section_inputs.shape[2]
    hidden = w_first.shape[1]
    zero_stat = jnp.zeros((stat_rows, hidden), jnp.float32)
    zero_rows = jnp.zeros((row_count, col_count), jnp.bfloat16)
    zero_units = jnp.zeros((row_count, hidden), jnp.float32)

    def project_in(current):
        return jnp.dot(current, w_first, preferred_element_type=jnp.float32)

    def project_back(current):
        return contract_last(current, w_second)

    def no_units(current):
        return zero_units

    def residual_forward(current, activation):
        return (
            current.astype(jnp.float32)
            + jnp.dot(activation, w_second, preferred_element_type=jnp.float32)
        ).astype(jnp.bfloat16)

    def residual_backward(current, slope):
        return (current.astype(jnp.float32) + contract_last(slope, w_first)).astype(jnp.bfloat16)

    def no_rows(current, other):
        return zero_rows

    def forward_step(state_carry, step_index):
        incoming, kept_x, kept_pre, kept_act = state_carry
        micro_index = step_index - section_index
        active = jnp.logical_and(micro_index >= 0, micro_index < micro_count)
        micro_slot = jnp.clip(micro_index, 0, micro_count - 1)
        own_rows = lax.dynamic_index_in_dim(section_inputs, micro_slot, 0, False)
        current = jnp.where(section_index == 0, own_rows, incoming)
        partial_value = lax.cond(active, project_in, no_units, current)
        preact, activation = combine_units(partial_value, unit_forward, zero_stat)
        result = lax.cond(active, residual_forward, no_rows, current, activation)
        kept_x = jnp.where(
            active, lax.dynamic_update_index_in_dim(kept_x, current, micro_slot, 0), kept_x
        )
        kept_pre = jnp.where(
            active, lax.dynamic_update_index_in_dim(kept_pre, preact, micro_slot, 0), kept_pre
        )
        kept_act = jnp.where(
            active, lax.dynamic_update_index_in_dim(kept_act, activation, micro_slot, 0), kept_act
        )
        outgoing = from_behind(result, "pipe", 1)
        return ((outgoing, kept_x, kept_pre, kept_act), None)

    forward_init = (
        zero_rows,
        jnp.zeros((micro_count, row_count, col_count), jnp.bfloat16),
        jnp.zeros((micro_count, stat_rows, hidden), jnp.float32),
        jnp.zeros((micro_count, row_count, hidden), jnp.bfloat16),
    )
    forward_final, unused_out = lax.scan(forward_step, forward_init, jnp.arange(step_count))
    unused_rows, kept_x, kept_pre, kept_act = forward_final

    def accumulate(state, x_part, act_part, err_part, slope_part):
        sum_in, err_in, sum_out, err_out = state
        x_groups = x_part.reshape(groups, -1, col_count)
        slope_groups = slope_part.reshape(groups, -1, hidden)
        act_groups = act_part.reshape(groups, -1, hidden)
        err_groups = err_part.reshape(groups, -1, col_count)
        grad_in = jnp.einsum(
            "gtc,gth->gch", x_groups, slope_groups, preferred_element_type=jnp.float32
        )
        grad_out = jnp.einsum(
            "gth,gtc->ghc", act_groups, err_groups, preferred_element_type=jnp.float32
        )
        sum_in, err_in = kahan_add(sum_in, err_in, grad_in)
        sum_out, err_out = kahan_add(sum_out, err_out, grad_out)
        return (sum_in, err_in, sum_out, err_out)

    def backward_step(state_carry, step_index):
        incoming, sums = state_carry
        micro_index = step_index - (sections - 1 - section_index)
        active = jnp.logical_and(micro_index >= 0, micro_index < micro_count)
        micro_slot = jnp.clip(micro_index, 0, micro_count - 1)
        own_rows = lax.dynamic_index_in_dim(section_seeds, micro_slot, 0, False)
        current = jnp.where(section_index == sections - 1, own_rows, incoming)
        partial_value = lax.cond(active, project_back, no_units, current)
        preact = lax.dynamic_index_in_dim(kept_pre, micro_slot, 0, False)
        unused_stat, slope = combine_units(partial_value, unit_backward, preact)
        x_here = lax.dynamic_index_in_dim(kept_x, micro_slot, 0, False)
        act_here = lax.dynamic_index_in_dim(kept_act, micro_slot, 0, False)
        sums = lax.cond(active, accumulate, keep_state, sums, x_here, act_here, current, slope)
        result = lax.cond(active, residual_backward, no_rows, current, slope)
        outgoing = from_behind(result, "pipe", -1)
        return ((outgoing, sums), None)

    sums_init = (
        jnp.zeros((groups, col_count, hidden), jnp.bfloat16),
        jnp.zeros((groups, col_count, hidden), jnp.bfloat16),
        jnp.zeros((groups, hidden, col_count), jnp.bfloat16),
        jnp.zeros((groups, hidden, col_count), jnp.bfloat16),
    )
    backward_final, unused_back = lax.scan(
        backward_step, (zero_rows, sums_init), jnp.arange(step_count)
    )
    unused_errors, final_sums = backward_final
    sum_in, err_in, sum_out, err_out = final_sums
    total_in = jnp.sum(sum_in.astype(jnp.float32) - err_in.astype(jnp.float32), axis=0)
    total_out = jnp.sum(sum_out.astype(jnp.float32) - err_out.astype(jnp.float32), axis=0)
    squares = jnp.sum(total_in * total_in) + jnp.sum(total_out * total_out)
    norm_squared = lax.psum(squares, ("pipe", "tensor", "dp"))
    grad_norm = jnp.sqrt(norm_squared)
    factor = jnp.minimum(1.0, CLIP_NORM / grad_norm)
    return ((total_in * factor)[None], (total_out * factor)[None], grad_norm)


def solution(mesh):
    in_specs = (
        P(None, "dp", "tensor"),
        P("pipe", ("tensor", "dp"), None),
        P("pipe", None, ("tensor", "dp")),
        P(None, "dp", "tensor"),
    )
    out_specs = (P("pipe", ("tensor", "dp"), None), P("pipe", None, ("tensor", "dp")), P())
    return jax.shard_map(
        on_device, mesh=mesh, in_specs=in_specs, out_specs=out_specs, check_vma=False
    )
```

profile of v0, /device:TPU:0, one launch (start us, length us, event | category | flops | bytes accessed | tf_op | source)
XLA Modules:
  0.0 1059.9 jit_solution(3159861756201324530)
XLA Ops:
  7.2 6.2 copy.17
  13.3 6.3 all-to-all-start.1
  19.7 6.2 copy.15
  25.8 42.0 %all-to-all-done.1 = bf16[2,128,4096]{1,0,2:T(2,128)(2,1)S(1)} async-done(((bf16[2,128,4096]{1,0,2:T(2,128)(2,1)}), bf16[2,128,4096]{1,0,2:T(2,128)(2,1)S(1)}, u32[]{:S(2)}, u32[]{:S(2)}) %all-to-all-start.1) | async-done | bytes 2097184 | tf_op jit(solution)/shard_map/all_to_all | solution.py:50
  76.2 43.9 %all-to-all-done = bf16[2,128,4096]{1,0,2:T(2,128)(2,1)} async-done(((bf16[2,128,4096]{1,0,2:T(2,128)(2,1)}), bf16[2,128,4096]{1,0,2:T(2,128)(2,1)}, u32[]{:S(2)}, u32[]{:S(2)}) %all-to-all-start) | async-done | bytes 2097184 | tf_op jit(solution)/shard_map/all_to_all | solution.py:51
  129.6 420.1 %while.37 = (s32[]{:T(128)}, bf16[512,1024]{1,0:T(8,128)(2,1)S(1)}, bf16[2,512,1024]{2,1,0:T(8,128)(2,1)}, f32[2,32,1024]{2,1,0:T(8,128)S(1)}, bf16[2,512,1024]{...) while((s32[]{:T(128)}, bf16[512,1024]{1,0:T(8,128)(2,1)S(1)}, ...), condition=%wide.region_6.7_spmd, body=%wide.region_0.6_spmd.sunk | while | flops 2150825984 | bytes 63570968 | solution.py:121
  139.1 60.1 %reduce-scatter.3.cloned.1.call-done = f32[32,1024]{1,0:T(8,128)} async-done(((f32[512,1024]{1,0:T(8,128)}), f32[32,1024]{1,0:T(8,128)}) %reduce-scatter.3.cloned.1.call-update) | async-done | bytes 131088 | tf_op jit(solution)/shard_map/while/body/eval_jaxpr/reduce_scatter | solution.py:57
  200.8 37.4 %all-gather.3.cloned.1.call-done = bf16[512,1024]{1,0:T(8,128)(2,1)} async-done(((bf16[32,1024]{1,0:T(8,128)(2,1)}), bf16[512,1024]{1,0:T(8,128)(2,1)}) %all-gather.3.cloned.1.call-update) | async-done | bytes 1048592 | tf_op jit(solution)/shard_map/while/body/eval_jaxpr/all_gather | solution.py:62
  245.8 21.6 %collective-permute-done = bf16[512,1024]{1,0:T(8,128)(2,1)S(1)} collective-permute-done((bf16[512,1024]{1,0:T(8,128)(2,1)}, bf16[512,1024]{1,0:T(8,128)(2,1)S(1)}, u32[]{:S(2)}, u32[]{:S(2)}) %collective-permute-start) | collective-permute-done | bytes 1048608 | tf_op jit(solution)/shard_map/while/body/eval_jaxpr/ppermute | solution.py:12
  276.8 61.8 %reduce-scatter.3.cloned.1.call-done = f32[32,1024]{1,0:T(8,128)} async-done(((f32[512,1024]{1,0:T(8,128)}), f32[32,1024]{1,0:T(8,128)}) %reduce-scatter.3.cloned.1.call-update) | async-done | bytes 131088 | tf_op jit(solution)/shard_map/while/body/eval_jaxpr/reduce_scatter | solution.py:57
  340.2 37.3 %all-gather.3.cloned.1.call-done = bf16[512,1024]{1,0:T(8,128)(2,1)} async-done(((bf16[32,1024]{1,0:T(8,128)(2,1)}), bf16[512,1024]{1,0:T(8,128)(2,1)}) %all-gather.3.cloned.1.call-update) | async-done | bytes 1048592 | tf_op jit(solution)/shard_map/while/body/eval_jaxpr/all_gather | solution.py:62
  387.2 21.3 %collective-permute-done = bf16[512,1024]{1,0:T(8,128)(2,1)S(1)} collective-permute-done((bf16[512,1024]{1,0:T(8,128)(2,1)}, bf16[512,1024]{1,0:T(8,128)(2,1)S(1)}, u32[]{:S(2)}, u32[]{:S(2)}) %collective-permute-start) | collective-permute-done | bytes 1048608 | tf_op jit(solution)/shard_map/while/body/eval_jaxpr/ppermute | solution.py:12
  415.0 64.7 %reduce-scatter.3.cloned.1.call-done = f32[32,1024]{1,0:T(8,128)} async-done(((f32[512,1024]{1,0:T(8,128)}), f32[32,1024]{1,0:T(8,128)}) %reduce-scatter.3.cloned.1.call-update) | async-done | bytes 131088 | tf_op jit(solution)/shard_map/while/body/eval_jaxpr/reduce_scatter | solution.py:57
  481.3 37.3 %all-gather.3.cloned.1.call-done = bf16[512,1024]{1,0:T(8,128)(2,1)} async-done(((bf16[32,1024]{1,0:T(8,128)(2,1)}), bf16[512,1024]{1,0:T(8,128)(2,1)}) %all-gather.3.cloned.1.call-update) | async-done | bytes 1048592 | tf_op jit(solution)/shard_map/while/body/eval_jaxpr/all_gather | solution.py:62
  519.7 6.9 collective-permute-start
  528.3 21.3 %collective-permute-done = bf16[512,1024]{1,0:T(8,128)(2,1)S(1)} collective-permute-done((bf16[512,1024]{1,0:T(8,128)(2,1)}, bf16[512,1024]{1,0:T(8,128)(2,1)S(1)}, u32[]{:S(2)}, u32[]{:S(2)}) %collective-permute-start) | collective-permute-done | bytes 1048608 | tf_op jit(solution)/shard_map/while/body/eval_jaxpr/ppermute | solution.py:12
  568.1 416.0 %while.38 = (s32[]{:T(128)}, bf16[512,1024]{1,0:T(8,128)(2,1)}, bf16[4,1024,1024]{2,1,0:T(8,128)(2,1)}, bf16[4,1024,1024]{2,1,0:T(8,128)(2,1)}, bf16[4,1024,1024...) while((s32[]{:T(128)}, bf16[512,1024]{1,0:T(8,128)(2,1)}, ...), condition=%wide.region_15.16_spmd, body=%wide.region_7.15_spmd.sunk | while | flops 4372856832 | bytes 124650128 | solution.py:163
  572.9 64.1 %reduce-scatter.5.cloned.1.call-done = f32[32,1024]{1,0:T(8,128)} async-done(((f32[512,1024]{1,0:T(8,128)}), f32[32,1024]{1,0:T(8,128)}) %reduce-scatter.5.cloned.1.call-update) | async-done | bytes 131088 | tf_op jit(solution)/shard_map/while/body/eval_jaxpr/reduce_scatter | solution.py:57
  638.5 37.4 %all-gather.5.cloned.1.call-done = bf16[512,1024]{1,0:T(8,128)(2,1)} async-done(((bf16[32,1024]{1,0:T(8,128)(2,1)}), bf16[512,1024]{1,0:T(8,128)(2,1)}) %all-gather.5.cloned.1.call-update) | async-done | bytes 1048592 | tf_op jit(solution)/shard_map/while/body/eval_jaxpr/all_gather | solution.py:62
  678.5 28.5 %collective-permute-done.1 = bf16[512,1024]{1,0:T(8,128)(2,1)} collective-permute-done((bf16[512,1024]{1,0:T(8,128)(2,1)}, bf16[512,1024]{1,0:T(8,128)(2,1)}, u32[]{:S(2)}, u32[]{:S(2)}) %collective-permute-start.1) | collective-permute-done | bytes 1048608 | tf_op jit(solution)/shard_map/while/body/eval_jaxpr/ppermute | solution.py:12
  714.3 61.0 %reduce-scatter.5.cloned.1.call-done = f32[32,1024]{1,0:T(8,128)} async-done(((f32[512,1024]{1,0:T(8,128)}), f32[32,1024]{1,0:T(8,128)}) %reduce-scatter.5.cloned.1.call-update) | async-done | bytes 131088 | tf_op jit(solution)/shard_map/while/body/eval_jaxpr/reduce_scatter | solution.py:57
  776.9 37.3 %all-gather.5.cloned.1.call-done = bf16[512,1024]{1,0:T(8,128)(2,1)} async-done(((bf16[32,1024]{1,0:T(8,128)(2,1)}), bf16[512,1024]{1,0:T(8,128)(2,1)}) %all-gather.5.cloned.1.call-update) | async-done | bytes 1048592 | tf_op jit(solution)/shard_map/while/body/eval_jaxpr/all_gather | solution.py:62
  819.8 24.7 %conditional.14 = ((bf16[4,1024,1024]{2,1,0:T(8,128)(2,1)}, bf16[4,1024,1024]{2,1,0:T(8,128)(2,1)}, bf16[4,1024,1024]{2,1,0:T(8,128)(2,1)}, bf16[4,1024,1024]{2,1,0:T(8,128)(2,1)})) conditional(s32[]{:T(128)} %convert_element_type.156, (bf16[4,1024,1024]{2,1,0:T(8,128)(2,1)}, bf16[4,1024,1024]{2,1,0:T(8,128)(2,1)}, ...), branch_computations={%region_13.13_spmd, %region_14.14_spmd} | conditional | flops 2222981120 | bytes 79691848 | solution.py:152
  821.4 11.5 %fusion.5 = (bf16[4,1024,1024]{2,1,0:T(8,128)(2,1)}, bf16[4,1024,1024]{2,1,0:T(8,128)(2,1)}) fusion(bf16[4,1024,1024]{2,1,0:T(8,128)(2,1)} %get-tuple-element.369, bf16[4,1024,1024]{2,1,0:T(8,128)(2,1)} %get-tuple-element.373, bf16[4,128,1024]{2,1,0:T(8,128)(2,1)S(1)} %bitcast.81, bf16[4,128,1024]{2,1,0:T(8,128)(2,1)S(1)} %bitcast.83), kind=kOutput, calls=%fused_computation.16 | convolution fusion | flops 1111490560 | bytes 35651584 | tf_op jit(solution)/shard_map/while/body/eval_jaxpr/cond/branch_1_fun/gtc,gth->gch/dot_general | solution.py:130
  832.9 11.6 %fusion.8 = (bf16[4,1024,1024]{2,1,0:T(8,128)(2,1)}, bf16[4,1024,1024]{2,1,0:T(8,128)(2,1)}) fusion(bf16[4,1024,1024]{2,1,0:T(8,128)(2,1)} %get-tuple-element.374, bf16[4,1024,1024]{2,1,0:T(8,128)(2,1)} %get-tuple-element.377, bf16[4,128,1024]{2,1,0:T(8,128)(2,1)S(1)} %bitcast.80, bf16[4,128,1024]{2,1,0:T(8,128)(2,1)S(1)} %bitcast.82), kind=kOutput, calls=%fused_computation.19 | convolution fusion | flops 1111490560 | bytes 35651584 | tf_op jit(solution)/shard_map/while/body/eval_jaxpr/cond/branch_1_fun/gth,gtc->ghc/dot_general | solution.py:133
  853.4 60.0 %reduce-scatter.5.cloned.1.call-done = f32[32,1024]{1,0:T(8,128)} async-done(((f32[512,1024]{1,0:T(8,128)}), f32[32,1024]{1,0:T(8,128)}) %reduce-scatter.5.cloned.1.call-update) | async-done | bytes 131088 | tf_op jit(solution)/shard_map/while/body/eval_jaxpr/reduce_scatter | solution.py:57
  915.0 37.3 %all-gather.5.cloned.1.call-done = bf16[512,1024]{1,0:T(8,128)(2,1)} async-done(((bf16[32,1024]{1,0:T(8,128)(2,1)}), bf16[512,1024]{1,0:T(8,128)(2,1)}) %all-gather.5.cloned.1.call-update) | async-done | bytes 1048592 | tf_op jit(solution)/shard_map/while/body/eval_jaxpr/all_gather | solution.py:62
  957.9 24.7 %conditional.14 = ((bf16[4,1024,1024]{2,1,0:T(8,128)(2,1)}, bf16[4,1024,1024]{2,1,0:T(8,128)(2,1)}, bf16[4,1024,1024]{2,1,0:T(8,128)(2,1)}, bf16[4,1024,1024]{2,1,0:T(8,128)(2,1)})) conditional(s32[]{:T(128)} %convert_element_type.156, (bf16[4,1024,1024]{2,1,0:T(8,128)(2,1)}, bf16[4,1024,1024]{2,1,0:T(8,128)(2,1)}, ...), branch_computations={%region_13.13_spmd, %region_14.14_spmd} | conditional | flops 2222981120 | bytes 79691848 | solution.py:152
  959.5 11.5 %fusion.5 = (bf16[4,1024,1024]{2,1,0:T(8,128)(2,1)}, bf16[4,1024,1024]{2,1,0:T(8,128)(2,1)}) fusion(bf16[4,1024,1024]{2,1,0:T(8,128)(2,1)} %get-tuple-element.369, bf16[4,1024,1024]{2,1,0:T(8,128)(2,1)} %get-tuple-element.373, bf16[4,128,1024]{2,1,0:T(8,128)(2,1)S(1)} %bitcast.81, bf16[4,128,1024]{2,1,0:T(8,128)(2,1)S(1)} %bitcast.83), kind=kOutput, calls=%fused_computation.16 | convolution fusion | flops 1111490560 | bytes 35651584 | tf_op jit(solution)/shard_map/while/body/eval_jaxpr/cond/branch_1_fun/gtc,gth->gch/dot_general | solution.py:130
  971.0 11.6 %fusion.8 = (bf16[4,1024,1024]{2,1,0:T(8,128)(2,1)}, bf16[4,1024,1024]{2,1,0:T(8,128)(2,1)}) fusion(bf16[4,1024,1024]{2,1,0:T(8,128)(2,1)} %get-tuple-element.374, bf16[4,1024,1024]{2,1,0:T(8,128)(2,1)} %get-tuple-element.377, bf16[4,128,1024]{2,1,0:T(8,128)(2,1)S(1)} %bitcast.80, bf16[4,128,1024]{2,1,0:T(8,128)(2,1)S(1)} %bitcast.82), kind=kOutput, calls=%fused_computation.19 | convolution fusion | flops 1111490560 | bytes 35651584 | tf_op jit(solution)/shard_map/while/body/eval_jaxpr/cond/branch_1_fun/gth,gtc->ghc/dot_general | solution.py:133
  984.1 14.6 %subtract_reduce_fusion = (f32[1024,1024]{1,0:T(8,128)S(1)}, f32[1024,1024]{1,0:T(8,128)S(1)}) fusion(bf16[4,1024,1024]{2,1,0:T(8,128)(2,1)} %get-tuple-element.414, bf16[4,1024,1024]{2,1,0:T(8,128)(2,1)} %get-tuple-element.413, bf16[4,1024,1024]{2,1,0:T(8,128)(2,1)} %get-tuple-element.412, bf16[4,1024,1024]{2,1,0:T(8,128)(2,1)} %get-tuple-element.411), kind=kLoop, calls=%fused_computation.33 | loop fusion | flops 31457280 | bytes 41943040 | tf_op jit(solution)/shard_map/reduce_sum | solution.py:169
  1005.3 38.2 %psum.7 = f32[]{:T(128)} all-reduce(f32[]{:T(128)S(6)} %add.61), channel_id=1, replica_groups=mesh['pipe'=2,'tensor'=4,'dp'=4] {'pipe','tensor','dp'}, use_global_device_ids=true, to_apply=%region_20.21 | all-reduce | flops 1 | bytes 8 | tf_op jit(solution)/shard_map/psum | solution.py:171
  (152 shorter events, 168.9 us)
Async XLA Ops:
  13.3 54.5 %all-to-all-start.1 = ((bf16[2,128,4096]{1,0,2:T(2,128)(2,1)}), bf16[2,128,4096]{1,0,2:T(2,128)(2,1)S(1)}, u32[]{:S(2)}, u32[]{:S(2)}) async-start(bf16[2,128,4096]{1,0,2:T(2,128)(2,1)} %copy.17), calls=%async_computation.3 | async-start | bytes 4194304 | tf_op jit(solution)/shard_map/all_to_all | solution.py:50
  67.9 52.3 %all-to-all-start = ((bf16[2,128,4096]{1,0,2:T(2,128)(2,1)}), bf16[2,128,4096]{1,0,2:T(2,128)(2,1)}, u32[]{:S(2)}, u32[]{:S(2)}) async-start(bf16[2,128,4096]{1,0,2:T(2,128)(2,1)} %copy.15), calls=%async_computation.2 | async-start | bytes 4194304 | tf_op jit(solution)/shard_map/all_to_all | solution.py:51
  129.6 69.6 %reduce-scatter.3.cloned.1.call-start = ((), (), s32[]{:S(2)}) async-start(), calls=%async_computation.4 | async-start | bytes 2228224 | tf_op jit(solution)/shard_map/while/body/eval_jaxpr/reduce_scatter | solution.py:57
  139.0 99.2 %all-gather.3.cloned.1.call-start = ((), (), s32[]{:S(2)}) async-start(), calls=%async_computation.5 | async-start | bytes 1114112 | tf_op jit(solution)/shard_map/while/body/eval_jaxpr/all_gather | solution.py:62
  238.2 5.9 copy-start.10
  238.2 5.9 copy-start.2
  242.8 24.7 %collective-permute-start = (bf16[512,1024]{1,0:T(8,128)(2,1)}, bf16[512,1024]{1,0:T(8,128)(2,1)S(1)}, u32[]{:S(2)}, u32[]{:S(2)}) collective-permute-start(bf16[512,1024]{1,0:T(8,128)(2,1)} %copy-done.9), channel_id=1, source_target_pairs={{0,16},{1,17},{2,18},{3,19},{4,20},{5,21},{6,22},{7,23},{8,24},{9,... | collective-permute-start | bytes 3145736 | tf_op jit(solution)/shard_map/while/body/eval_jaxpr/ppermute | solution.py:12
  245.8 21.6 %copy-start.3 = (bf16[2,512,1024]{2,1,0:T(8,128)(2,1)}, bf16[2,512,1024]{2,1,0:T(8,128)(2,1)S(1)}, u32[]{:S(2)}) copy-start(bf16[2,512,1024]{2,1,0:T(8,128)(2,1)S(1)} %fusion.37) | copy-start | bytes 6291460 | tf_op jit(solution)/shard_map/while
  267.4 71.2 %reduce-scatter.3.cloned.1.call-start = ((), (), s32[]{:S(2)}) async-start(), calls=%async_computation.4 | async-start | bytes 2228224 | tf_op jit(solution)/shard_map/while/body/eval_jaxpr/reduce_scatter | solution.py:57
  276.8 100.8 %all-gather.3.cloned.1.call-start = ((), (), s32[]{:S(2)}) async-start(), calls=%async_computation.5 | async-start | bytes 1114112 | tf_op jit(solution)/shard_map/while/body/eval_jaxpr/all_gather | solution.py:62
  377.5 8.0 copy-start.10
  377.5 8.0 copy-start.2
  382.1 26.5 %collective-permute-start = (bf16[512,1024]{1,0:T(8,128)(2,1)}, bf16[512,1024]{1,0:T(8,128)(2,1)S(1)}, u32[]{:S(2)}, u32[]{:S(2)}) collective-permute-start(bf16[512,1024]{1,0:T(8,128)(2,1)} %copy-done.9), channel_id=1, source_target_pairs={{0,16},{1,17},{2,18},{3,19},{4,20},{5,21},{6,22},{7,23},{8,24},{9,... | collective-permute-start | bytes 3145736 | tf_op jit(solution)/shard_map/while/body/eval_jaxpr/ppermute | solution.py:12
  387.2 21.3 %copy-start.3 = (bf16[2,512,1024]{2,1,0:T(8,128)(2,1)}, bf16[2,512,1024]{2,1,0:T(8,128)(2,1)S(1)}, u32[]{:S(2)}) copy-start(bf16[2,512,1024]{2,1,0:T(8,128)(2,1)S(1)} %fusion.37) | copy-start | bytes 6291460 | tf_op jit(solution)/shard_map/while
  408.5 71.2 %reduce-scatter.3.cloned.1.call-start = ((), (), s32[]{:S(2)}) async-start(), calls=%async_computation.4 | async-start | bytes 2228224 | tf_op jit(solution)/shard_map/while/body/eval_jaxpr/reduce_scatter | solution.py:57
  415.0 103.7 %all-gather.3.cloned.1.call-start = ((), (), s32[]{:S(2)}) async-start(), calls=%async_computation.5 | async-start | bytes 1114112 | tf_op jit(solution)/shard_map/while/body/eval_jaxpr/all_gather | solution.py:62
  518.6 8.0 copy-start.10
  518.6 8.0 copy-start.2
  519.7 29.9 %collective-permute-start = (bf16[512,1024]{1,0:T(8,128)(2,1)}, bf16[512,1024]{1,0:T(8,128)(2,1)S(1)}, u32[]{:S(2)}, u32[]{:S(2)}) collective-permute-start(bf16[512,1024]{1,0:T(8,128)(2,1)} %copy-done.9), channel_id=1, source_target_pairs={{0,16},{1,17},{2,18},{3,19},{4,20},{5,21},{6,22},{7,23},{8,24},{9,... | collective-permute-start | bytes 3145736 | tf_op jit(solution)/shard_map/while/body/eval_jaxpr/ppermute | solution.py:12
  528.3 21.3 %copy-start.3 = (bf16[2,512,1024]{2,1,0:T(8,128)(2,1)}, bf16[2,512,1024]{2,1,0:T(8,128)(2,1)S(1)}, u32[]{:S(2)}) copy-start(bf16[2,512,1024]{2,1,0:T(8,128)(2,1)S(1)} %fusion.37) | copy-start | bytes 6291460 | tf_op jit(solution)/shard_map/while
  568.1 68.8 %reduce-scatter.5.cloned.1.call-start = ((), (), s32[]{:S(2)}) async-start(), calls=%async_computation.6 | async-start | bytes 2228224 | tf_op jit(solution)/shard_map/while/body/eval_jaxpr/reduce_scatter | solution.py:57
  572.8 103.2 %all-gather.5.cloned.1.call-start = ((), (), s32[]{:S(2)}) async-start(), calls=%async_computation.7 | async-start | bytes 1114112 | tf_op jit(solution)/shard_map/while/body/eval_jaxpr/all_gather | solution.py:62
  677.1 29.8 %collective-permute-start.1 = (bf16[512,1024]{1,0:T(8,128)(2,1)}, bf16[512,1024]{1,0:T(8,128)(2,1)}, u32[]{:S(2)}, u32[]{:S(2)}) collective-permute-start(bf16[512,1024]{1,0:T(8,128)(2,1)} %get-tuple-element.754), channel_id=1, source_target_pairs={{16,0},{17,1},{18,2},{19,3},{20,4},{21,5},{22,6},{23,7},{24,8},{25... | collective-permute-start | bytes 3145736 | tf_op jit(solution)/shard_map/while/body/eval_jaxpr/ppermute | solution.py:12
  706.9 68.3 %reduce-scatter.5.cloned.1.call-start = ((), (), s32[]{:S(2)}) async-start(), calls=%async_computation.6 | async-start | bytes 2228224 | tf_op jit(solution)/shard_map/while/body/eval_jaxpr/reduce_scatter | solution.py:57
  714.3 99.9 %all-gather.5.cloned.1.call-start = ((), (), s32[]{:S(2)}) async-start(), calls=%async_computation.7 | async-start | bytes 1114112 | tf_op jit(solution)/shard_map/while/body/eval_jaxpr/all_gather | solution.py:62
  814.2 5.6 copy-start.4
  818.5 27.5 %collective-permute-start.1 = (bf16[512,1024]{1,0:T(8,128)(2,1)}, bf16[512,1024]{1,0:T(8,128)(2,1)}, u32[]{:S(2)}, u32[]{:S(2)}) collective-permute-start(bf16[512,1024]{1,0:T(8,128)(2,1)} %get-tuple-element.754), channel_id=1, source_target_pairs={{16,0},{17,1},{18,2},{19,3},{20,4},{21,5},{22,6},{23,7},{24,8},{25... | collective-permute-start | bytes 3145736 | tf_op jit(solution)/shard_map/while/body/eval_jaxpr/ppermute | solution.py:12
  846.0 67.3 %reduce-scatter.5.cloned.1.call-start = ((), (), s32[]{:S(2)}) async-start(), calls=%async_computation.6 | async-start | bytes 2228224 | tf_op jit(solution)/shard_map/while/body/eval_jaxpr/reduce_scatter | solution.py:57
  853.4 98.9 %all-gather.5.cloned.1.call-start = ((), (), s32[]{:S(2)}) async-start(), calls=%async_computation.7 | async-start | bytes 1114112 | tf_op jit(solution)/shard_map/while/body/eval_jaxpr/all_gather | solution.py:62
  952.3 5.6 copy-start.4
  956.6 27.5 %collective-permute-start.1 = (bf16[512,1024]{1,0:T(8,128)(2,1)}, bf16[512,1024]{1,0:T(8,128)(2,1)}, u32[]{:S(2)}, u32[]{:S(2)}) collective-permute-start(bf16[512,1024]{1,0:T(8,128)(2,1)} %get-tuple-element.754), channel_id=1, source_target_pairs={{16,0},{17,1},{18,2},{19,3},{20,4},{21,5},{22,6},{23,7},{24,8},{25... | collective-permute-start | bytes 3145736 | tf_op jit(solution)/shard_map/while/body/eval_jaxpr/ppermute | solution.py:12
  1044.3 5.2 copy-start.7
  (14 other events, 22.1 us)
Sparse Core Ops, SparseCore 0:
  139.1 60.0 reduce-scatter.2
  201.4 36.7 all-gather.2
  276.9 61.6 reduce-scatter.2
  340.7 36.7 all-gather.2
  415.1 64.6 reduce-scatter.2
  481.8 36.7 all-gather.2
  572.9 63.9 reduce-scatter.4
  639.1 36.8 all-gather.4
  714.4 60.8 reduce-scatter.4
  777.4 36.7 all-gather.4
  853.5 59.8 reduce-scatter.4
  915.4 36.7 all-gather.4
where the time goes:
time: 1060 us
  waiting for transfers between devices  778 us (73%)
  matrix products  74.1 us (7%)
  local copies, waits for them, and re-layouts  65.6 us (6%)
  other arithmetic  55.8 us (5%)
  blocking collectives  38.2 us (4%)
  starting transfers between devices  26.6 us (3%)
  between operations  17.2 us (2%)
    reduce_scatter x6, waiting for transfers between devices, combine_units(): lax.psum_scatter(partial_value, ('tensor', 'dp'), scatter_dimension=0, ti...  372 us
    all_gather x6, waiting for transfers between devices, combine_units(): lax.all_gather(unit_fn(share_part, kept_stat), ('tensor', 'dp'), axis=0,...  224 us
    ppermute x6, waiting for transfers between devices, from_behind(): return lax.ppermute(value, axis, pairs)  95.7 us
    all_to_all x1, waiting for transfers between devices, on_device(): lax.all_to_all(cotangent, 'dp', split_axis=2, concat_axis=1, tiled=True)  43.9 us
    all_to_all x1, waiting for transfers between devices, on_device(): lax.all_to_all(inputs, 'dp', split_axis=2, concat_axis=1, tiled=True)  42 us
    psum x1, blocking collectives, on_device(): norm_squared = lax.psum(squares, ('pipe', 'tensor', 'dp'))  38.2 us
    dot_general x2, matrix products, accumulate(): jnp.einsum('gth,gtc->ghc', act_groups, err_groups, preferred_element_type...  23.1 us
    dot_general x2, matrix products, accumulate(): jnp.einsum('gtc,gth->gch', x_groups, slope_groups, preferred_element_type...  23.1 us
  transfers between devices with their start and end apart: 20, of which 20 were waited for; matrix products, arithmetic and copies ran while one was open for 6% of the time, Pallas kernels for 0%

commit v1 on v0

v1 whole, which is shorter than its diff:
```python
import jax
import jax.numpy as jnp
from jax import lax
from jax.sharding import PartitionSpec as P

CLIP_NORM = 16384
BF = jnp.bfloat16
F32 = jnp.float32
PLANE = ("tensor", "dp")


def mm(a, b, ca, cb):
    return lax.dot_general(a, b, (((ca,), (cb,)), ((), ())), preferred_element_type=F32)


def swap_pipe(value):
    return lax.ppermute(value, "pipe", [(0, 1), (1, 0)])


def chain(a0, a1, u1, u0, g):
    act0 = jax.nn.silu(a0).astype(BF)
    pre1 = a1 + mm(act0, g, 1, 0)
    sig1 = jax.nn.sigmoid(pre1)
    act1 = (pre1 * sig1).astype(BF)
    slope1 = (u1 * sig1 * (1.0 + pre1 * (1.0 - sig1))).astype(BF)
    up0 = u0 + mm(slope1, g, 1, 1)
    sig0 = jax.nn.sigmoid(a0)
    slope0 = (up0 * sig0 * (1.0 + a0 * (1.0 - sig0))).astype(BF)
    return act0, act1, slope1, slope0


def on_device(inputs, w_in, w_out, cotangent):
    first = lax.axis_index("pipe") == 0
    a_own = w_in[0]
    b_own = w_out[0].T
    hidden = a_own.shape[1]
    v_other = swap_pipe(jnp.where(first, b_own, a_own))
    mine = lax.all_to_all(
        jnp.where(first, inputs, cotangent), "dp", split_axis=2, concat_axis=1, tiled=True
    )
    mine = mine.reshape(-1, mine.shape[-1])
    v_own = jnp.where(first, a_own, b_own)

    g_left = jnp.where(first, b_own, v_other)
    g_right = jnp.where(first, v_other, a_own)
    g_part = mm(g_left, g_right, 0, 0).astype(BF)
    g_share = lax.psum_scatter(g_part, PLANE, scatter_dimension=0, tiled=True)
    g = lax.all_gather(g_share, PLANE, axis=0, tiled=True)

    part = jnp.concatenate([mm(mine, v_own, 1, 0), mm(mine, v_other, 1, 0)], axis=1).astype(BF)
    share = lax.psum_scatter(part, PLANE, scatter_dimension=0, tiled=True)
    share_other = swap_pipe(share)
    other = swap_pipe(mine)
    pre_pair = jnp.where(first, share, share_other).astype(F32)
    up_pair = jnp.where(first, share_other, share).astype(F32)
    act0, act1, slope1, slope0 = chain(
        pre_pair[:, :hidden], pre_pair[:, hidden:], up_pair[:, :hidden], up_pair[:, hidden:], g
    )
    send = jnp.concatenate(
        [
            jnp.where(first, slope1, act0),
            jnp.where(first, act0, act1),
            jnp.where(first, slope0, slope1),
        ],
        axis=1,
    )
    full = lax.all_gather(send, PLANE, axis=0, tiled=True)
    relay, act, slope = full[:, :hidden], full[:, hidden : 2 * hidden], full[:, 2 * hidden :]
    moved = (other.astype(F32) + mm(relay, v_other, 1, 1)).astype(BF)
    x_here = jnp.where(first, mine, moved)
    err_here = jnp.where(first, moved, mine)
    total_in = mm(x_here, slope, 0, 0)
    total_out = mm(act, err_here, 0, 0)
    squares = jnp.sum(total_in * total_in) + jnp.sum(total_out * total_out)
    grad_norm = jnp.sqrt(lax.psum(squares, ("pipe", "tensor", "dp")))
    factor = jnp.minimum(1.0, CLIP_NORM / grad_norm)
    return ((total_in * factor)[None], (total_out * factor)[None], grad_norm)


def solution(mesh):
    in_specs = (
        P(None, "dp", "tensor"),
        P("pipe", ("tensor", "dp"), None),
        P("pipe", None, ("tensor", "dp")),
        P(None, "dp", "tensor"),
    )
    out_specs = (P("pipe", ("tensor", "dp"), None), P("pipe", None, ("tensor", "dp")), P())
    return jax.shard_map(
        on_device, mesh=mesh, in_specs=in_specs, out_specs=out_specs, check_vma=False
    )
```

time: 1060 us -> 389 us (0.37)
  waiting for transfers between devices: 778 us -> 242 us
  matrix products: 74.1 us -> 31.9 us
  local copies, waits for them, and re-layouts: 65.6 us -> 27.9 us
  other arithmetic: 55.8 us -> 19.3 us
  starting transfers between devices: 26.6 us -> 11.1 us
    reduce_scatter x6 -> x2, waiting for transfers between devices: 372 us -> 101 us  [the longest x1 75.9 us: on_device(): share = lax.psum_scatter(part, PLANE, scatter_dimension=0, tiled=True)]
    all_gather x6 -> x2, waiting for transfers between devices: 224 us -> 47.3 us  [the longest x1 34.9 us: on_device(): g = lax.all_gather(g_share, PLANE, axis=0, tiled=True)]
    all_to_all x2 -> x1, waiting for transfers between devices: 86 us -> 16.3 us  [on_device(): lax.all_to_all(jnp.where(first, inputs, cotangent), 'dp', split_axis=2, c...]
    dot_general x12 -> x8, matrix products: 74.1 us -> 31.9 us  [mm(): lax.dot_general(a, b, (((ca,), (cb,)), ((), ())), preferred_element_type=...]
    another operation x6 -> x0, local copies, waits for them, and re-layouts: 20.4 us -> none
    ppermute x6 -> x3, waiting for transfers between devices: 95.7 us -> 77.3 us  [swap_pipe(): return lax.ppermute(value, 'pipe', [(0, 1), (1, 0)])]
    reduce_sum x3 -> x0, other arithmetic: 17.9 us -> none  [the longest x1 14.6 us: on_device(): jnp.sum(sum_out.astype(jnp.float32) - err_out.astype(jnp.float32), axis=0)]
    select_n x12 -> x2, other arithmetic: 20.8 us -> 6.25 us  [the longest x1 3.13 us: on_device(): jnp.where(first, inputs, cotangent)]
  transfers between devices with their start and end apart: 20 -> 8, of which waited for: 20 -> 8; matrix products, arithmetic and copies ran while one was open for 6% -> 12% of each run, Pallas kernels for 0% -> 0%
where the time goes in v1:
time: 389 us; the launch traced here: 388 us
  waiting for transfers between devices  242 us (62%)
  blocking collectives  39.2 us (10%)
  matrix products  31.9 us (8%)
  local copies, waits for them, and re-layouts  27.9 us (7%)
  other arithmetic  19.3 us (5%)
  between operations  17 us (4%)
  starting transfers between devices  11.1 us (3%)
    ppermute x3, waiting for transfers between devices, swap_pipe(): return lax.ppermute(value, 'pipe', [(0, 1), (1, 0)])  77.3 us
    reduce_scatter x1, waiting for transfers between devices, on_device(): share = lax.psum_scatter(part, PLANE, scatter_dimension=0, tiled=True)  75.9 us
    psum x1, blocking collectives, on_device(): grad_norm = jnp.sqrt(lax.psum(squares, ('pipe', 'tensor', 'dp')))  39.2 us
    all_gather x1, waiting for transfers between devices, on_device(): g = lax.all_gather(g_share, PLANE, axis=0, tiled=True)  34.9 us
    dot_general x8, matrix products, mm(): lax.dot_general(a, b, (((ca,), (cb,)), ((), ())), preferred_element_type=...  31.9 us
    reduce_scatter x1, waiting for transfers between devices, on_device(): g_share = lax.psum_scatter(g_part, PLANE, scatter_dimension=0, tiled=True)  24.6 us
    unnamed x14, local copies, waits for them, and re-layouts  21.6 us
    all_to_all x1, waiting for transfers between devices, on_device(): lax.all_to_all(jnp.where(first, inputs, cotangent), 'dp', split_axis=2, c...  16.3 us
  transfers between devices with their start and end apart: 8, of which 8 were waited for; matrix products, arithmetic and copies ran while one was open for 12% of the time, Pallas kernels for 0%

profile of v1, /device:TPU:0, one launch (start us, length us, event | category | flops | bytes accessed | tf_op | source)
XLA Modules:
  0.0 387.9 jit_solution(4626085157356654505)
XLA Ops:
  7.2 2.9 copy.14
  10.0 3.1 bitcast_select_fusion.1
  13.2 3.0 collective-permute-start.1
  16.1 6.2 %copy.11 = bf16[2,128,4096]{1,0,2:T(2,128)(2,1)} copy(bf16[2,128,4096]{2,1,0:T(8,128)(2,1)} %param.4) | data formatting | bytes 4194304 | tf_op args[0]
  22.3 6.2 %copy.12 = bf16[2,128,4096]{1,0,2:T(2,128)(2,1)} copy(bf16[2,128,4096]{2,1,0:T(8,128)(2,1)} %param.7) | data formatting | bytes 4194304 | tf_op args[3]
  28.5 3.1 broadcast_select_fusion
  31.6 4.9 %all-to-all-start = ((bf16[2,128,4096]{1,0,2:T(2,128)(2,1)}), bf16[2,128,4096]{1,0,2:T(2,128)(2,1)}, u32[]{:S(2)}, u32[]{:S(2)}) async-start(bf16[2,128,4096]{1,0,2:T(2,128)(2,1)} %bitcast.43), calls=%async_computation | async-start | bytes 4194304 | tf_op jit(solution)/shard_map/all_to_all | solution.py:38
  36.5 25.6 %collective-permute-done.1 = bf16[1024,1024]{1,0:T(8,128)(2,1)} collective-permute-done((bf16[1024,1024]{1,0:T(8,128)(2,1)}, bf16[1024,1024]{1,0:T(8,128)(2,1)}, u32[]{:S(2)}, u32[]{:S(2)}) %collective-permute-start.1) | collective-permute-done | bytes 2097184 | tf_op jit(solution)/shard_map/ppermute | solution.py:17
  62.1 6.0 %fusion.15 = bf16[1024,1024]{1,0:T(8,128)(2,1)} fusion(bf16[1024,1024]{1,0:T(8,128)(2,1)} %collective-permute-done.1, bf16[1,1024,1024]{2,1,0:T(8,128)(2,1)} %param.5, pred[]{:T(512)S(6)} %eq.3, bf16[1,1024,1024]{1,2,0:T(8,128)(2,1)S(1)} %copy.14), kind=kOutput, calls=%fused_computation.26 | convolution fusion | flops 2150629376 | bytes 8388609 | tf_op jit(solution)/shard_map/dot_general | solution.py:13
  68.2 16.3 %all-to-all-done = bf16[2,128,4096]{1,0,2:T(2,128)(2,1)} async-done(((bf16[2,128,4096]{1,0,2:T(2,128)(2,1)}), bf16[2,128,4096]{1,0,2:T(2,128)(2,1)}, u32[]{:S(2)}, u32[]{:S(2)}) %all-to-all-start) | async-done | bytes 2097184 | tf_op jit(solution)/shard_map/all_to_all | solution.py:38
  84.5 6.2 %copy.13 = bf16[2,128,4,1024]{3,1,2,0:T(8,128)(2,1)} copy(bf16[2,128,4,1024]{1,0,3,2:T(2,128)(2,1)} %bitcast) | data formatting | bytes 4194304 | tf_op jit(solution)/shard_map/all_to_all | solution.py:38
  90.7 4.8 %convolution_convert_fusion = bf16[1024,1024]{0,1:T(8,128)(2,1)S(1)} fusion(bf16[1024,1024]{1,0:T(8,128)(2,1)} %bitcast.46, bf16[1024,1024]{1,0:T(8,128)(2,1)} %collective-permute-done.1), kind=kOutput, calls=%fused_computation.28 | convolution fusion | flops 2148532224 | bytes 6291456 | tf_op jit(solution)/shard_map/dot_general | solution.py:13
  95.5 2.5 fusion.16
  98.0 2.5 pad_maximum_fusion
  100.5 6.4 %copy.18 = bf16[1024,2048]{1,0:T(8,128)(2,1)} copy(bf16[1024,2048]{0,1:T(8,128)(2,1)} %pad_maximum_fusion) | data formatting | bytes 8388608
  107.0 24.6 %reduce-scatter.5.cloned.1.call-done = bf16[64,1024]{1,0:T(8,128)(2,1)} async-done(((bf16[1024,1024]{1,0:T(8,128)(2,1)}), bf16[64,1024]{1,0:T(8,128)(2,1)}) %reduce-scatter.5.cloned.1.call-update) | async-done | bytes 131088 | tf_op jit(solution)/shard_map/reduce_scatter | solution.py:47
  131.8 75.9 %reduce-scatter.7.cloned.1.call-done = bf16[64,2048]{1,0:T(8,128)(2,1)} async-done(((bf16[1024,2048]{1,0:T(8,128)(2,1)}), bf16[64,2048]{1,0:T(8,128)(2,1)}) %reduce-scatter.7.cloned.1.call-update) | async-done | bytes 262160 | tf_op jit(solution)/shard_map/reduce_scatter | solution.py:51
  207.8 1.5 collective-permute-start.2
  209.2 5.3 %collective-permute-done.2 = bf16[64,2048]{1,0:T(8,128)(2,1)S(1)} collective-permute-done((bf16[64,2048]{1,0:T(8,128)(2,1)}, bf16[64,2048]{1,0:T(8,128)(2,1)S(1)}, u32[]{:S(2)}, u32[]{:S(2)}) %collective-permute-start.2) | collective-permute-done | bytes 262176 | tf_op jit(solution)/shard_map/ppermute | solution.py:17
  214.5 1.0 select_convert_fusion.1
  215.6 34.9 %all-gather.3.cloned.1.call-done = bf16[1024,1024]{1,0:T(8,128)(2,1)} async-done(((bf16[64,1024]{1,0:T(8,128)(2,1)}), bf16[1024,1024]{1,0:T(8,128)(2,1)}) %all-gather.3.cloned.1.call-update) | async-done | bytes 2097168 | tf_op jit(solution)/shard_map/all_gather | solution.py:48
  250.5 2.3 broadcast_select_fusion.2
  252.8 0.8 broadcast_select_fusion.1
  253.6 0.8 pad_maximum_fusion.1
  254.4 1.5 collective-permute-start
  256.0 46.4 %collective-permute-done = bf16[1024,1024]{1,0:T(8,128)(2,1)} collective-permute-done((bf16[1024,1024]{1,0:T(8,128)(2,1)S(1)}, bf16[1024,1024]{1,0:T(8,128)(2,1)}, u32[]{:S(2)}, u32[]{:S(2)}) %collective-permute-start) | collective-permute-done | bytes 2097184 | tf_op jit(solution)/shard_map/ppermute | solution.py:17
  302.4 12.3 %all-gather.5.cloned.1.call-done = bf16[1024,3072]{1,0:T(8,128)(2,1)} async-done(((bf16[64,3072]{1,0:T(8,128)(2,1)}), bf16[1024,3072]{1,0:T(8,128)(2,1)}) %all-gather.5.cloned.1.call-update) | async-done | bytes 6291472 | tf_op jit(solution)/shard_map/all_gather | solution.py:67
  314.7 5.4 %add_convert_fusion = bf16[1024,1024]{1,0:T(8,128)(2,1)S(1)} fusion(bf16[1024,1024]{1,0:T(8,128)(2,1)} %collective-permute-done, bf16[1024,1024]{1,0:T(8,128)(2,1)} %collective-permute-done.1, bf16[1024,3072]{1,0:T(8,128)(2,1)} %all-gather.5.cloned.1.call-done), kind=kOutput, calls=%fused_computation.5 | convolution fusion | flops 2150629376 | bytes 8388608 | tf_op jit(solution)/shard_map/dot_general | solution.py:13
  320.1 5.0 %multiply_reduce_fusion = (f32[]{:T(128)}, f32[1024,1024]{1,0:T(8,128)}) fusion(bf16[1024,1024]{1,0:T(8,128)(2,1)S(1)} %add_convert_fusion, bf16[1024,1024]{1,0:T(8,128)(2,1)S(1)} %bitcast.49, pred[]{:T(512)S(6)} %eq.3, bf16[1024,3072]{1,0:T(8,128)(2,1)S(1)} %copy-done.3), kind=kOutput, calls=%fused_computation.3 | convolution fusion | flops 2150629376 | bytes 10485765 | tf_op jit(solution)/shard_map/dot_general | solution.py:13
  325.1 5.1 %multiply_reduce_fusion.1 = (f32[]{:T(128)}, f32[1024,1024]{1,0:T(8,128)}) fusion(bf16[1024,3072]{1,0:T(8,128)(2,1)S(1)} %copy-done.3, bf16[1024,1024]{1,0:T(8,128)(2,1)S(1)} %bitcast.50, bf16[1024,1024]{1,0:T(8,128)(2,1)S(1)} %add_convert_fusion, pred[]{:T(512)S(6)} %eq.3), kind=kOutput, calls=%fused_computation.4 | convolution fusion | flops 2150629376 | bytes 10485765 | tf_op jit(solution)/shard_map/dot_general | solution.py:13
  331.5 39.2 %psum.7 = f32[]{:T(128)} all-reduce(f32[]{:T(128)S(6)} %add.39), channel_id=1, replica_groups=mesh['pipe'=2,'tensor'=4,'dp'=4] {'pipe','tensor','dp'}, use_global_device_ids=true, to_apply=%region_4.5 | all-reduce | flops 1 | bytes 8 | tf_op jit(solution)/shard_map/psum | solution.py:75
  371.5 8.8 %multiply_bitcast_fusion = (f32[1,1024,1024]{2,1,0:T(8,128)}, f32[1,1024,1024]{2,1,0:T(8,128)}) fusion(f32[1024,1024]{1,0:T(8,128)} %get-tuple-element.11, f32[]{:T(128)S(6)} %min.3, f32[1024,1024]{1,0:T(8,128)} %get-tuple-element.9), kind=kLoop, calls=%fused_computation.1 | loop fusion | flops 2097152 | bytes 16777220 | tf_op jit(solution)/shard_map/broadcast_in_dim | solution.py:77
  (18 shorter events, 0.4 us)
Async XLA Ops:
  13.2 48.9 %collective-permute-start.1 = (bf16[1024,1024]{1,0:T(8,128)(2,1)}, bf16[1024,1024]{1,0:T(8,128)(2,1)}, u32[]{:S(2)}, u32[]{:S(2)}) collective-permute-start(bf16[1024,1024]{1,0:T(8,128)(2,1)} %bitcast_select_fusion.1), channel_id=1, source_target_pairs={{0,16},{16,0},{1,17},{17,1},{2,18},{18,2},{3,19},{19,3},{4,20},{20... | collective-permute-start | bytes 6291464 | tf_op jit(solution)/shard_map/ppermute | solution.py:17
  31.6 52.9 %all-to-all-start = ((bf16[2,128,4096]{1,0,2:T(2,128)(2,1)}), bf16[2,128,4096]{1,0,2:T(2,128)(2,1)}, u32[]{:S(2)}, u32[]{:S(2)}) async-start(bf16[2,128,4096]{1,0,2:T(2,128)(2,1)} %bitcast.43), calls=%async_computation | async-start | bytes 4194304 | tf_op jit(solution)/shard_map/all_to_all | solution.py:38
  36.5 95.1 %reduce-scatter.5.cloned.1.call-start = ((), (), s32[]{:S(2)}) async-start(), calls=%async_computation.3 | async-start | bytes 2228224 | tf_op jit(solution)/shard_map/reduce_scatter | solution.py:47
  68.1 139.6 %reduce-scatter.7.cloned.1.call-start = ((), (), s32[]{:S(2)}) async-start(), calls=%async_computation.6 | async-start | bytes 4456448 | tf_op jit(solution)/shard_map/reduce_scatter | solution.py:51
  90.7 4.8 %copy-start = (bf16[1,1024,1024]{2,1,0:T(8,128)(2,1)S(1)}, bf16[1,1024,1024]{2,1,0:T(8,128)(2,1)}, u32[]{:S(2)}) copy-start(bf16[1,1024,1024]{2,1,0:T(8,128)(2,1)} %param.5) | copy-start | bytes 6291460
  90.7 4.8 %copy-start.1 = (bf16[2,128,4,1024]{3,1,2,0:T(8,128)(2,1)S(1)}, bf16[2,128,4,1024]{3,1,2,0:T(8,128)(2,1)}, u32[]{:S(2)}) copy-start(bf16[2,128,4,1024]{3,1,2,0:T(8,128)(2,1)} %copy.13) | copy-start | bytes 6291460
  106.9 143.6 %all-gather.3.cloned.1.call-start = ((), (), s32[]{:S(2)}) async-start(), calls=%async_computation.4 | async-start | bytes 2228224 | tf_op jit(solution)/shard_map/all_gather | solution.py:48
  131.6 183.1 %all-gather.5.cloned.1.call-start = ((), (), s32[]{:S(2)}) async-start(), calls=%async_computation.5 | async-start | bytes 6684672 | tf_op jit(solution)/shard_map/all_gather | solution.py:67
  207.8 6.8 %collective-permute-start.2 = (bf16[64,2048]{1,0:T(8,128)(2,1)}, bf16[64,2048]{1,0:T(8,128)(2,1)S(1)}, u32[]{:S(2)}, u32[]{:S(2)}) collective-permute-start(bf16[64,2048]{1,0:T(8,128)(2,1)} %reduce-scatter.7.cloned.1.call-done), channel_id=1, source_target_pairs={{0,16},{16,0},{1,17},{17,1},{2,18},{18,2},{3,19},{19,3},{4,20},{20... | collective-permute-start | bytes 786440 | tf_op jit(solution)/shard_map/ppermute | solution.py:17
  250.5 2.3 copy-start.4
  252.8 1.6 copy-start.2
  254.4 47.9 %collective-permute-start = (bf16[1024,1024]{1,0:T(8,128)(2,1)S(1)}, bf16[1024,1024]{1,0:T(8,128)(2,1)}, u32[]{:S(2)}, u32[]{:S(2)}) collective-permute-start(bf16[1024,1024]{1,0:T(8,128)(2,1)S(1)} %bitcast.48), channel_id=1, source_target_pairs={{0,16},{16,0},{1,17},{17,1},{2,18},{18,2},{3,19},{19,3},{4,20},{20... | collective-permute-start | bytes 6291464 | tf_op jit(solution)/shard_map/ppermute | solution.py:17
  314.7 5.4 %copy-start.3 = (bf16[1024,3072]{1,0:T(8,128)(2,1)S(1)}, bf16[1024,3072]{1,0:T(8,128)(2,1)}, u32[]{:S(2)}) copy-start(bf16[1024,3072]{1,0:T(8,128)(2,1)} %all-gather.5.cloned.1.call-done) | copy-start | bytes 18874372
Sparse Core Ops, SparseCore 0:
  68.3 63.2 reduce-scatter.4
  136.0 71.6 reduce-scatter.6
  210.0 40.4 all-gather.2
  254.5 60.1 all-gather.4

commit v2 on v1

--- a/solution.py
+++ b/solution.py
@@ -1,12 +1,346 @@
 import jax
 import jax.numpy as jnp
 from jax import lax
+from jax.experimental import pallas as pl
+from jax.experimental.pallas import tpu as pltpu
 from jax.sharding import PartitionSpec as P
 
 CLIP_NORM = 16384
 BF = jnp.bfloat16
 F32 = jnp.float32
-PLANE = ("tensor", "dp")
+
+
+WIDTH = 512
+BLOCK = 64
+MESH = pl.DeviceIdType.MESH
+
+
+def place():
+    return tuple(lax.axis_index(name) for name in ("pipe", "tensor", "dp"))
+
+
+def plane_peers():
+    p, t, d = place()
+    levels = lax.axis_size("tensor").bit_length() - 1
+    count = lax.axis_size("dp")
+    partners = []
+    for level in range(levels):
+        bit = 1 << level
+        flipped = t + bit - 2 * bit * lax.rem(t // bit, 2)
+        partners.append((p, flipped, d))
+    ring = [(p, t, lax.rem(d + off, count)) for off in range(1, count)]
+    back = [(p, t, lax.rem(d + count - off, count)) for off in range(1, count)]
+    return partners, ring, back
+
+
+def meet(peers):
+    barrier = pltpu.get_barrier_semaphore()
+    for peer in peers:
+        pl.semaphore_signal(barrier, inc=1, device_id=peer, device_id_type=MESH)
+    pl.semaphore_wait(barrier, len(peers))
+
+
+def chunks_of(shapes):
+    return [
+        (item, pl.ds(col, min(WIDTH, shape[1])))
+        for item, shape in enumerate(shapes)
+        for col in range(0, shape[1], min(WIDTH, shape[1]))
+    ]
+
+
+def over_rows(rows, body):
+    block = min(BLOCK, rows)
+
+    def step(index, carry):
+        body(pl.multiple_of(index * block, block), block)
+        return carry
+
+    lax.fori_loop(0, rows // block, step, 0)
+
+
+def remote(src, dst, send_sem, recv_sem, peer):
+    return pltpu.make_async_remote_copy(
+        src_ref=src,
+        dst_ref=dst,
+        send_sem=send_sem,
+        recv_sem=recv_sem,
+        device_id=peer,
+        device_id_type=MESH,
+    )
+
+
+def reduce_rows(parts, out_types, collective_id):
+    shapes = [part.shape for part in parts]
+    items = len(parts)
+    levels = lax.axis_size("tensor").bit_length() - 1
+    count = lax.axis_size("dp")
+    ways = count << levels
+    chunks = chunks_of(shapes)
+
+    def kernel(*refs):
+        ins, outs = refs[:items], refs[items : 2 * items]
+        rest = refs[2 * items :]
+        recvs = [rest[item * levels : (item + 1) * levels] for item in range(items)]
+        rest = rest[items * levels :]
+        sums = [rest[item * levels : (item + 1) * levels] for item in range(items)]
+        rest = rest[items * levels :]
+        lands = rest[:items]
+        send_sem, recv_sem, ring_send, ring_recv = rest[items:]
+        p, t, d = place()
+        partners, ring, back = plane_peers()
+        meet(partners + ring)
+        sent = []
+
+        def start(copy):
+            copy.start()
+            sent.append(copy)
+            return copy
+
+        def half(level, item):
+            bit = lax.rem(t // (1 << level), 2)
+            rows = shapes[item][0] >> (level + 1)
+            return pl.multiple_of(bit * rows, rows), pl.multiple_of((1 - bit) * rows, rows), rows
+
+        def exchange(level, slot):
+            item, cols = chunks[slot]
+            keep, give, rows = half(level, item)
+            source = ins[item] if level == 0 else sums[item][level - 1]
+            return start(
+                remote(
+                    source.at[pl.ds(give, rows), cols],
+                    recvs[item][level].at[:, cols],
+                    send_sem.at[level, slot],
+                    recv_sem.at[level, slot],
+                    partners[level],
+                )
+            )
+
+        flight = [exchange(0, slot) for slot in range(len(chunks))]
+        ringed = [None] * len(chunks)
+        for level in range(levels):
+            following = []
+            for slot, (item, cols) in enumerate(chunks):
+                keep, give, rows = half(level, item)
+                source = ins[item] if level == 0 else sums[item][level - 1]
+                flight[slot].wait_recv()
+
+                def add(row, block, source=source, item=item, cols=cols, keep=keep):
+                    left = source[pl.ds(pl.multiple_of(keep + row, block), block), cols]
+                    right = recvs[item][level][pl.ds(row, block), cols]
+                    total = left.astype(F32) + right.astype(F32)
+                    sums[item][level][pl.ds(row, block), cols] = total.astype(BF)
+
+                over_rows(rows, add)
+                if level + 1 < levels:
+                    following.append(exchange(level + 1, slot))
+                else:
+                    share = shapes[item][0] // ways
+                    ringed[slot] = [
+                        start(
+                            remote(
+                                sums[item][level].at[
+                                    pl.ds(pl.multiple_of(peer[2] * share, share), share), cols
+                                ],
+                                lands[item].at[off, :, cols],
+                                ring_send.at[off, slot],
+                                ring_recv.at[off, slot],
+                                peer,
+                            )
+                        )
+                        for off, peer in enumerate(ring)
+                    ]
+            flight = following
+        for slot, (item, cols) in enumerate(chunks):
+            share = shapes[item][0] // ways
+            for copy in ringed[slot]:
+                copy.wait_recv()
+
+            def finish(row, block, item=item, cols=cols, share=share):
+                mine = pl.multiple_of(d * share + row, block)
+                total = sums[item][levels - 1][pl.ds(mine, block), cols].astype(F32)
+                for off in range(count - 1):
+                    total = total + lands[item][off, pl.ds(row, block), cols].astype(F32)
+                outs[item][pl.ds(row, block), cols] = total.astype(outs[item].dtype)
+
+            over_rows(share, finish)
+        for copy in sent:
+            copy.wait_send()
+
+    vmem = pl.BlockSpec(memory_space=pltpu.VMEM)
+    halves = [
+        pltpu.VMEM((shape[0] >> (level + 1), shape[1]), BF)
+        for shape in shapes
+        for level in range(levels)
+    ]
+    lands = [pltpu.VMEM((count - 1, shape[0] // ways, shape[1]), BF) for shape in shapes]
+    dma = pltpu.SemaphoreType.DMA
+    size = sum(part.size for part in parts)
+    return pl.pallas_call(
+        kernel,
+        out_shape=[
+            jax.ShapeDtypeStruct((shape[0] // ways, shape[1]), kind)
+            for shape, kind in zip(shapes, out_types)
+        ],
+        in_specs=[vmem] * items,
+        out_specs=[vmem] * items,
+        scratch_shapes=halves
+        + halves
+        + lands
+        + [
+            dma((levels, len(chunks))),
+            dma((levels, len(chunks))),
+            dma((count - 1, len(chunks))),
+            dma((count - 1, len(chunks))),
+        ],
+        compiler_params=pltpu.CompilerParams(
+            collective_id=collective_id, has_side_effects=True, vmem_limit_bytes=64_000_000
+        ),
+        cost_estimate=pl.CostEstimate(flops=size, bytes_accessed=size * 40, transcendentals=0),
+        name="reduce_rows",
+    )(*parts)
+
+
+def gather_rows(share_array, collective_id):
+    share, width = share_array.shape
+    levels = lax.axis_size("tensor").bit_length() - 1
+    count = lax.axis_size("dp")
+    rows_all = (share * count) << levels
+    chunks = chunks_of([(rows_all, width)])
+
+    def kernel(in_ref, out_ref, send_sem, recv_sem, ring_send, ring_recv, own_sem):
+        p, t, d = place()
+        partners, ring, back = plane_peers()
+        meet(partners + ring)
+        sent = []
+
+        def start(copy):
+            copy.start()
+            sent.append(copy)
+            return copy
+
+        begin = [0]
+        for level in range(levels):
+            begin.append(begin[-1] + lax.rem(t // (1 << level), 2) * (rows_all >> (level + 1)))
+        mine = pl.ds(pl.multiple_of(begin[levels] + d * share, share), share)
+        local = pltpu.make_async_copy(in_ref, out_ref.at[mine, :], own_sem)
+        local.start()
+        flight = [
+            [
+                start(
+                    remote(
+                        in_ref.at[:, cols],
+                        out_ref.at[mine, cols],
+                        ring_send.at[off, slot],
+                        ring_recv.at[off, slot],
+                        peer,
+                    )
+                )
+                for off, peer in enumerate(ring)
+            ]
+            for slot, (item, cols) in enumerate(chunks)
+        ]
+        local.wait()
+        for level in reversed(range(levels)):
+            rows = rows_all >> (level + 1)
+            piece = pl.ds(pl.multiple_of(begin[level + 1], rows), rows)
+            following = []
+            for slot, (item, cols) in enumerate(chunks):
+                for copy in flight[slot]:
+                    copy.wait_recv()
+                following.append(
+                    [
+                        start(
+                            remote(
+                                out_ref.at[piece, cols],
+                                out_ref.at[piece, cols],
+                                send_sem.at[level, slot],
+                                recv_sem.at[level, slot],
+                                partners[level],
+                            )
+                        )
+                    ]
+                )
+            flight = following
+        for copies in flight:
+            for copy in copies:
+                copy.wait_recv()
+        for copy in sent:
+            copy.wait_send()
+
+    dma = pltpu.SemaphoreType.DMA
+    size = rows_all * width
+    return pl.pallas_call(
+        kernel,
+        out_shape=jax.ShapeDtypeStruct((rows_all, width), BF),
+        in_specs=[pl.BlockSpec(memory_space=pltpu.VMEM)],
+        out_specs=pl.BlockSpec(memory_space=pl.ANY),
+        scratch_shapes=[
+            dma((levels, len(chunks))),
+            dma((levels, len(chunks))),
+            dma((count - 1, len(chunks))),
+            dma((count - 1, len(chunks))),
+            dma,
+        ],
+        compiler_params=pltpu.CompilerParams(collective_id=collective_id, has_side_effects=True),
+        cost_estimate=pl.CostEstimate(flops=size, bytes_accessed=size * 40, transcendentals=0),
+        name="gather_rows",
+    )(share_array)
+
+
+def sum_all(value, collective_id):
+    sizes = [lax.axis_size(name) for name in ("pipe", "tensor", "dp")]
+    total = sizes[0] * sizes[1] * sizes[2]
+
+    def kernel(in_ref, out_ref, land, send_sem, recv_sem):
+        p, t, d = place()
+        me = (p * sizes[1] + t) * sizes[2] + d
+
+        def peer_of(off):
+            there = lax.rem(me + off, total)
+            return (
+                there // (sizes[1] * sizes[2]),
+                lax.rem(there // sizes[2], sizes[1]),
+                lax.rem(there, sizes[2]),
+            )
+
+        def copy_of(off):
+            return remote(
+                in_ref, land.at[off - 1], send_sem.at[off - 1], recv_sem.at[off - 1], peer_of(off)
+            )
+
+        barrier = pltpu.get_barrier_semaphore()
+
+        def greet(off, carry):
+            pl.semaphore_signal(barrier, inc=1, device_id=peer_of(off), device_id_type=MESH)
+            return carry
+
+        lax.fori_loop(1, total, greet, 0)
+        pl.semaphore_wait(barrier, total - 1)
+
+        def send(off, carry):
+            copy_of(off).start()
+            return carry
+
+        lax.fori_loop(1, total, send, 0)
+
+        def receive(off, carry):
+            copy_of(off).wait()
+            return carry
+
+        lax.fori_loop(1, total, receive, 0)
+        out_ref[...] = in_ref[...] + jnp.sum(land[...], axis=0)
+
+    vmem = pl.BlockSpec(memory_space=pltpu.VMEM)
+    dma = pltpu.SemaphoreType.DMA
+    return pl.pallas_call(
+        kernel,
+        out_shape=jax.ShapeDtypeStruct((8, 128), F32),
+        in_specs=[vmem],
+        out_specs=vmem,
+        scratch_shapes=[pltpu.VMEM((total - 1, 8, 128), F32), dma((total - 1,)), dma((total - 1,))],
+        compiler_params=pltpu.CompilerParams(collective_id=collective_id, has_side_effects=True),
+        name="sum_all",
+    )(jnp.full((8, 128), value, F32))[0, 0]
 
 
 def mm(a, b, ca, cb):
@@ -44,15 +378,14 @@
     g_left = jnp.where(first, b_own, v_other)
     g_right = jnp.where(first, v_other, a_own)
     g_part = mm(g_left, g_right, 0, 0).astype(BF)
-    g_share = lax.psum_scatter(g_part, PLANE, scatter_dimension=0, tiled=True)
-    g = lax.all_gather(g_share, PLANE, axis=0, tiled=True)
 
     part = jnp.concatenate([mm(mine, v_own, 1, 0), mm(mine, v_other, 1, 0)], axis=1).astype(BF)
-    share = lax.psum_scatter(part, PLANE, scatter_dimension=0, tiled=True)
-    share_other = swap_pipe(share)
+    g_share, share = reduce_rows([g_part, part], [BF, F32], 0)
+    g = gather_rows(g_share, 1)
+    share_other = swap_pipe(share.astype(BF)).astype(F32)
     other = swap_pipe(mine)
-    pre_pair = jnp.where(first, share, share_other).astype(F32)
-    up_pair = jnp.where(first, share_other, share).astype(F32)
+    pre_pair = jnp.where(first, share, share_other)
+    up_pair = jnp.where(first, share_other, share)
     act0, act1, slope1, slope0 = chain(
         pre_pair[:, :hidden], pre_pair[:, hidden:], up_pair[:, :hidden], up_pair[:, hidden:], g
     )
@@ -64,7 +397,7 @@
         ],
         axis=1,
     )
-    full = lax.all_gather(send, PLANE, axis=0, tiled=True)
+    full = gather_rows(send, 2)
     relay, act, slope = full[:, :hidden], full[:, hidden : 2 * hidden], full[:, 2 * hidden :]
     moved = (other.astype(F32) + mm(relay, v_other, 1, 1)).astype(BF)
     x_here = jnp.where(first, mine, moved)
@@ -72,7 +405,7 @@
     total_in = mm(x_here, slope, 0, 0)
     total_out = mm(act, err_here, 0, 0)
     squares = jnp.sum(total_in * total_in) + jnp.sum(total_out * total_out)
-    grad_norm = jnp.sqrt(lax.psum(squares, ("pipe", "tensor", "dp")))
+    grad_norm = jnp.sqrt(sum_all(squares, 3))
     factor = jnp.minimum(1.0, CLIP_NORM / grad_norm)
     return ((total_in * factor)[None], (total_out * factor)[None], grad_norm)
 

time: 389 us -> 278 us (0.71)
  waiting for transfers between devices: 242 us -> 45.4 us
  Pallas kernels: 0 us -> 144 us
  blocking collectives: 39.2 us -> 0 us
  between operations: 17 us -> 3.97 us
  local copies, waits for them, and re-layouts: 27.9 us -> 23 us
    pallas_call x0 -> x4, Pallas kernels: none -> 144 us  [the longest x2 79.5 us: gather_rows(): pl.pallas_call(kernel, out_shape=jax.ShapeDtypeStruct((rows_all, width),...]
    reduce_scatter x2 -> x0, waiting for transfers between devices: 101 us -> none  [the longest x1 75.9 us: on_device(): share = lax.psum_scatter(part, PLANE, scatter_dimension=0, tiled=True)]
    all_gather x2 -> x0, waiting for transfers between devices: 47.3 us -> none  [the longest x1 34.9 us: on_device(): g = lax.all_gather(g_share, PLANE, axis=0, tiled=True)]
    psum x1 -> x0, blocking collectives: 39.2 us -> none  [on_device(): grad_norm = jnp.sqrt(lax.psum(squares, ('pipe', 'tensor', 'dp')))]
    ppermute x3, waiting for transfers between devices: 77.3 us -> 45.4 us  [swap_pipe(): return lax.ppermute(value, 'pipe', [(0, 1), (1, 0)])]
    all_to_all x1, waiting for transfers between devices: 16.3 us -> 0.01 us  [on_device(): lax.all_to_all(jnp.where(first, inputs, cotangent), 'dp', split_axis=2, c...]
    unnamed x14 -> x17, local copies, waits for them, and re-layouts: 21.6 us -> 15.1 us
  transfers between devices with their start and end apart: 8 -> 4, of which waited for: 8 -> 1; matrix products, arithmetic and copies ran while one was open for 12% -> 7% of each run, Pallas kernels for 0% -> 47%
where the time goes in v2:
time: 278 us; the launch traced here: 277 us
  Pallas kernels  144 us (52%)
  waiting for transfers between devices  45.4 us (16%)
  matrix products  31.9 us (11%)
  local copies, waits for them, and re-layouts  23 us (8%)
  other arithmetic  16.7 us (6%)
  starting transfers between devices  11.6 us (4%)
  between operations  3.97 us (1%)
    pallas_call x2, Pallas kernels, gather_rows(): pl.pallas_call(kernel, out_shape=jax.ShapeDtypeStruct((rows_all, width),...  79.5 us
    pallas_call x1, Pallas kernels, reduce_rows(): pl.pallas_call(kernel, out_shape=[jax.ShapeDtypeStruct((shape[0] // ways,...  50.8 us
    ppermute x3, waiting for transfers between devices, swap_pipe(): return lax.ppermute(value, 'pipe', [(0, 1), (1, 0)])  45.4 us
    dot_general x8, matrix products, mm(): lax.dot_general(a, b, (((ca,), (cb,)), ((), ())), preferred_element_type=...  31.9 us
    unnamed x17, local copies, waits for them, and re-layouts  15.1 us
    pallas_call x1, Pallas kernels, sum_all(): pl.pallas_call(kernel, out_shape=jax.ShapeDtypeStruct((8, 128), F32), in_...  14.1 us
    broadcast_in_dim x1, other arithmetic, on_device(): return ((total_in * factor)[None], (total_out * factor)[None], grad_norm)  8.78 us
    all_to_all x1, starting transfers between devices, on_device(): lax.all_to_all(jnp.where(first, inputs, cotangent), 'dp', split_axis=2, c...  6.35 us
  transfers between devices with their start and end apart: 4, of which 1 were waited for; matrix products, arithmetic and copies ran while one was open for 7% of the time, Pallas kernels for 47%

profile of v2, /device:TPU:0, one launch (start us, length us, event | category | flops | bytes accessed | tf_op | source)
XLA Modules:
  0.0 277.1 jit_solution(16281162442324141174)
XLA Ops:
  0.6 4.7 %copy.11 = bf16[2,128,4096]{1,0,2:T(2,128)(2,1)S(1)} copy(bf16[2,128,4096]{2,1,0:T(8,128)(2,1)} %param.4) | data formatting | bytes 4194304 | tf_op args[0]
  5.4 6.2 %copy.12 = bf16[2,128,4096]{1,0,2:T(2,128)(2,1)} copy(bf16[2,128,4096]{2,1,0:T(8,128)(2,1)} %param.7) | data formatting | bytes 4194304 | tf_op args[3]
  11.5 1.5 broadcast_select_fusion
  13.1 6.3 %all-to-all-start = ((bf16[2,128,4096]{1,0,2:T(2,128)(2,1)}), bf16[2,128,4096]{1,0,2:T(2,128)(2,1)}, u32[]{:S(2)}, u32[]{:S(2)}) async-start(bf16[2,128,4096]{1,0,2:T(2,128)(2,1)} %bitcast.42), calls=%async_computation | async-start | bytes 4194304 | tf_op jit(solution)/shard_map/all_to_all | solution.py:372
  19.4 2.9 %copy.14 = bf16[1,1024,1024]{1,2,0:T(8,128)(2,1)S(1)} copy(bf16[1,1024,1024]{2,1,0:T(8,128)(2,1)} %param.6) | data formatting | bytes 4194304 | tf_op args[2]
  22.3 0.0 copy-start.1
  22.3 2.0 bitcast_select_fusion.2
  24.3 3.1 %collective-permute-start.1 = (bf16[1024,1024]{1,0:T(8,128)(2,1)S(1)}, bf16[1024,1024]{1,0:T(8,128)(2,1)S(1)}, u32[]{:S(2)}, u32[]{:S(2)}) collective-permute-start(bf16[1024,1024]{1,0:T(8,128)(2,1)S(1)} %bitcast_select_fusion.2), channel_id=1, source_target_pairs={{0,16},{16,0},{1,17},{17,1},{2,18},{18,2},{3,19},{19,3},{4,20},{20... | collective-permute-start | bytes 6291464 | tf_op jit(solution)/shard_map/ppermute | solution.py:351
  27.4 45.3 %collective-permute-done.1 = bf16[1024,1024]{1,0:T(8,128)(2,1)S(1)} collective-permute-done((bf16[1024,1024]{1,0:T(8,128)(2,1)S(1)}, bf16[1024,1024]{1,0:T(8,128)(2,1)S(1)}, u32[]{:S(2)}, u32[]{:S(2)}) %collective-permute-start.1) | collective-permute-done | bytes 2097184 | tf_op jit(solution)/shard_map/ppermute | solution.py:351
  72.8 1.3 copy-done.4
  74.1 3.8 %fusion.16.refs_0_ = bf16[1024,1024]{1,0:T(8,128)(2,1)} fusion(bf16[1024,1024]{1,0:T(8,128)(2,1)S(1)} %collective-permute-done.1, bf16[1,1024,1024]{2,1,0:T(8,128)(2,1)S(1)} %copy-done.1, pred[]{:T(512)S(6)} %eq.3, bf16[1,1024,1024]{1,2,0:T(8,128)(2,1)S(1)} %copy.14), kind=kOutput, calls=%fused_computation.27 | convolution fusion | flops 2150629376 | bytes 8388609 | tf_op jit(solution)/shard_map/dot_general | solution.py:347
  77.9 6.2 %copy.13 = bf16[2,128,4,1024]{3,1,2,0:T(8,128)(2,1)} copy(bf16[2,128,4,1024]{1,0,3,2:T(2,128)(2,1)} %bitcast) | data formatting | bytes 4194304 | tf_op jit(solution)/shard_map/all_to_all | solution.py:372
  84.0 4.7 %fusion.15 = bf16[1024,1024]{1,0:T(8,128)(2,1)S(1)} fusion(bf16[1024,1024]{1,0:T(8,128)(2,1)} %bitcast.2, bf16[1,1024,1024]{2,1,0:T(8,128)(2,1)} %param.5, bf16[1,1024,1024]{1,2,0:T(8,128)(2,1)S(1)} %copy.14, pred[]{:T(512)S(6)} %eq.3), kind=kOutput, calls=%fused_computation.26 | convolution fusion | flops 2149580800 | bytes 8388609 | tf_op jit(solution)/shard_map/dot_general | solution.py:347
  88.8 1.8 collective-permute-start
  90.6 4.0 %convolution_convert_fusion = bf16[1024,1024]{1,0:T(8,128)(2,1)S(1)} fusion(bf16[1024,1024]{1,0:T(8,128)(2,1)} %bitcast.2, bf16[1024,1024]{1,0:T(8,128)(2,1)S(1)} %copy-done.5), kind=kOutput, calls=%fused_computation.28 | convolution fusion | flops 2148532224 | bytes 6291456 | tf_op jit(solution)/shard_map/dot_general | solution.py:347
  94.5 2.5 pad_maximum_fusion.refs_1_
  97.0 50.8 %reduce_rows.1 = (bf16[64,1024]{1,0:T(8,128)(2,1)}, f32[64,2048]{1,0:T(8,128)}) custom-call(bf16[1024,1024]{1,0:T(8,128)(2,1)} %fusion.16.refs_0_, bf16[1024,2048]{1,0:T(8,128)(2,1)} %pad_maximum_fusion.refs_1_), custom_call_target="tpu_custom_call" | custom-call | flops 3145728 | bytes 125829120 | tf_op jit(solution)/shard_map/reduce_rows/pallas_call | solution.py:178
  147.9 1.1 convert_element_type.30
  149.0 0.3 collective-permute-start.2
  149.3 24.8 %gather_rows.2 = bf16[1024,1024]{1,0:T(8,128)(2,1)} custom-call(bf16[64,1024]{1,0:T(8,128)(2,1)} %get-tuple-element.6.in_ref), custom_call_target="tpu_custom_call" | custom-call | flops 1048576 | bytes 41943040 | tf_op jit(solution)/shard_map/gather_rows/pallas_call | solution.py:272
  174.1 0.1 convert_select_fusion.1
  174.3 2.3 broadcast_select_fusion.2
  176.6 0.8 broadcast_select_fusion.1
  177.4 0.8 pad_maximum_fusion.1.in_ref
  178.2 54.7 %gather_rows.3 = bf16[1024,3072]{1,0:T(8,128)(2,1)} custom-call(bf16[64,3072]{1,0:T(8,128)(2,1)} %pad_maximum_fusion.1.in_ref), custom_call_target="tpu_custom_call" | custom-call | flops 3145728 | bytes 125829120 | tf_op jit(solution)/shard_map/gather_rows/pallas_call | solution.py:272
  232.9 4.7 %add_convert_fusion = bf16[1024,1024]{1,0:T(8,128)(2,1)S(1)} fusion(bf16[1024,1024]{1,0:T(8,128)(2,1)} %collective-permute-done, bf16[1024,1024]{1,0:T(8,128)(2,1)S(1)} %copy-done.6, bf16[1024,3072]{1,0:T(8,128)(2,1)} %gather_rows.3), kind=kOutput, calls=%fused_computation.5 | convolution fusion | flops 2150629376 | bytes 8388608 | tf_op jit(solution)/shard_map/dot_general | solution.py:347
  237.7 5.0 %multiply_reduce_fusion = (f32[]{:T(128)}, f32[1024,1024]{1,0:T(8,128)}) fusion(bf16[1024,1024]{1,0:T(8,128)(2,1)S(1)} %add_convert_fusion, bf16[1024,1024]{1,0:T(8,128)(2,1)} %bitcast.2, pred[]{:T(512)S(6)} %eq.3, bf16[1024,3072]{1,0:T(8,128)(2,1)S(1)} %copy-done), kind=kOutput, calls=%fused_computation.3 | convolution fusion | flops 2150629376 | bytes 10485765 | tf_op jit(solution)/shard_map/dot_general | solution.py:347
  242.7 6.6 %multiply_reduce_fusion.1 = (f32[]{:T(128)}, f32[1024,1024]{1,0:T(8,128)}) fusion(bf16[1024,3072]{1,0:T(8,128)(2,1)S(1)} %copy-done, bf16[1024,1024]{1,0:T(8,128)(2,1)} %bitcast.2, bf16[1024,1024]{1,0:T(8,128)(2,1)S(1)} %add_convert_fusion, pred[]{:T(512)S(6)} %eq.3), kind=kOutput, calls=%fused_computation.4 | convolution fusion | flops 2150629376 | bytes 10485765 | tf_op jit(solution)/shard_map/dot_general | solution.py:347
  250.6 0.6 broadcast_in_dim.9.in_ref
  251.2 14.1 %sum_all.1 = f32[8,128]{1,0:T(8,128)} custom-call(f32[8,128]{1,0:T(8,128)} %broadcast_in_dim.9.in_ref), custom_call_target="tpu_custom_call" | custom-call | tf_op jit(solution)/shard_map/sum_all/pallas_call | solution.py:335
  265.3 1.2 slice.31
  267.2 8.8 %multiply_bitcast_fusion = (f32[1,1024,1024]{2,1,0:T(8,128)}, f32[1,1024,1024]{2,1,0:T(8,128)}) fusion(f32[1024,1024]{1,0:T(8,128)} %get-tuple-element.15, f32[]{:T(128)S(6)} %min.3, f32[1024,1024]{1,0:T(8,128)} %get-tuple-element.13), kind=kLoop, calls=%fused_computation.1 | loop fusion | flops 2097152 | bytes 16777220 | tf_op jit(solution)/shard_map/broadcast_in_dim | solution.py:410
  (15 shorter events, 0.0 us)
Async XLA Ops:
  13.1 64.8 %all-to-all-start = ((bf16[2,128,4096]{1,0,2:T(2,128)(2,1)}), bf16[2,128,4096]{1,0,2:T(2,128)(2,1)}, u32[]{:S(2)}, u32[]{:S(2)}) async-start(bf16[2,128,4096]{1,0,2:T(2,128)(2,1)} %bitcast.42), calls=%async_computation | async-start | bytes 4194304 | tf_op jit(solution)/shard_map/all_to_all | solution.py:372
  22.3 51.8 %copy-start.1 = (bf16[1,1024,1024]{2,1,0:T(8,128)(2,1)S(1)}, bf16[1,1024,1024]{2,1,0:T(8,128)(2,1)}, u32[]{:S(2)}) copy-start(bf16[1,1024,1024]{2,1,0:T(8,128)(2,1)} %param.5) | copy-start | bytes 6291460
  24.3 48.5 %collective-permute-start.1 = (bf16[1024,1024]{1,0:T(8,128)(2,1)S(1)}, bf16[1024,1024]{1,0:T(8,128)(2,1)S(1)}, u32[]{:S(2)}, u32[]{:S(2)}) collective-permute-start(bf16[1024,1024]{1,0:T(8,128)(2,1)S(1)} %bitcast_select_fusion.2), channel_id=1, source_target_pairs={{0,16},{16,0},{1,17},{17,1},{2,18},{18,2},{3,19},{19,3},{4,20},{20... | collective-permute-start | bytes 6291464 | tf_op jit(solution)/shard_map/ppermute | solution.py:351
  72.7 1.3 copy-start.4
  84.0 6.5 %copy-start.5 = (bf16[1024,1024]{1,0:T(8,128)(2,1)S(1)}, bf16[1024,1024]{1,0:T(8,128)(2,1)}, u32[]{:S(2)}) copy-start(bf16[1024,1024]{1,0:T(8,128)(2,1)} %copy-done.4) | copy-start | bytes 6291460
  88.8 144.2 %collective-permute-start = (bf16[1024,1024]{1,0:T(8,128)(2,1)}, bf16[1024,1024]{1,0:T(8,128)(2,1)}, u32[]{:S(2)}, u32[]{:S(2)}) collective-permute-start(bf16[1024,1024]{1,0:T(8,128)(2,1)} %bitcast.2), channel_id=1, source_target_pairs={{0,16},{16,0},{1,17},{17,1},{2,18},{18,2},{3,19},{19,3},{4,20},{20... | collective-permute-start | bytes 6291464 | tf_op jit(solution)/shard_map/ppermute | solution.py:351
  147.8 26.3 %copy-start.3 = (f32[64,2048]{1,0:T(8,128)S(1)}, f32[64,2048]{1,0:T(8,128)}, u32[]{:S(2)}) copy-start(f32[64,2048]{1,0:T(8,128)} %get-tuple-element.5) | copy-start | bytes 1572868
  149.0 25.1 %collective-permute-start.2 = (bf16[64,2048]{1,0:T(8,128)(2,1)S(1)}, bf16[64,2048]{1,0:T(8,128)(2,1)S(1)}, u32[]{:S(2)}, u32[]{:S(2)}) collective-permute-start(bf16[64,2048]{1,0:T(8,128)(2,1)S(1)} %convert_element_type.30), channel_id=1, source_target_pairs={{0,16},{16,0},{1,17},{17,1},{2,18},{18,2},{3,19},{19,3},{4,20},{20... | collective-permute-start | bytes 786440 | tf_op jit(solution)/shard_map/ppermute | solution.py:351
  174.3 2.3 copy-start.2
  178.2 54.8 %copy-start.6 = (bf16[1024,1024]{1,0:T(8,128)(2,1)S(1)}, bf16[1024,1024]{1,0:T(8,128)(2,1)}, u32[]{:S(2)}) copy-start(bf16[1024,1024]{1,0:T(8,128)(2,1)} %copy-done.4) | copy-start | bytes 6291460
  232.9 4.8 %copy-start = (bf16[1024,3072]{1,0:T(8,128)(2,1)S(1)}, bf16[1024,3072]{1,0:T(8,128)(2,1)}, u32[]{:S(2)}) copy-start(bf16[1024,3072]{1,0:T(8,128)(2,1)} %gather_rows.3) | copy-start | bytes 18874372

commit v3 on v2

--- a/solution.py
+++ b/solution.py
@@ -10,7 +10,7 @@
 F32 = jnp.float32
 
 
-WIDTH = 512
+WIDTH = 256
 BLOCK = 64
 MESH = pl.DeviceIdType.MESH
 
@@ -343,6 +343,75 @@
     )(jnp.full((8, 128), value, F32))[0, 0]
 
 
+def spread(inputs, cotangent, weight, collective_id):
+    count = lax.axis_size("dp")
+    batches, tokens, width = inputs.shape
+    part = width // count
+
+    def kernel(in_ref, cot_ref, w_ref, out_ref, far_ref, send_sem, recv_sem, w_send, w_recv, own_sem):
+        p, t, d = place()
+        partners, ring, back = plane_peers()
+        across = (1 - p, t, d)
+        meet(ring + [across])
+
+        def columns(index):
+            return pl.ds(pl.multiple_of(index * part, part), part)
+
+        def copies_of(source):
+            return [
+                remote(
+                    source.at[:, :, columns(peer[2])],
+                    out_ref.at[d],
+                    send_sem.at[off],
+                    recv_sem.at[off],
+                    peer,
+                )
+                for off, peer in enumerate(ring)
+            ]
+
+        def own_of(source):
+            return pltpu.make_async_copy(source.at[:, :, columns(d)], out_ref.at[d], own_sem)
+
+        def begin(source):
+            for copy in copies_of(source):
+                copy.start()
+            own_of(source).start()
+
+        weights = remote(w_ref, far_ref, w_send, w_recv, across)
+        weights.start()
+
+        @pl.when(p == 0)
+        def _():
+            begin(in_ref)
+
+        @pl.when(p != 0)
+        def _():
+            begin(cot_ref)
+
+        for copy in copies_of(in_ref):
+            copy.wait()
+        own_of(in_ref).wait()
+        weights.wait()
+
+    anywhere = pl.BlockSpec(memory_space=pl.ANY)
+    dma = pltpu.SemaphoreType.DMA
+    return pl.pallas_call(
+        kernel,
+        out_shape=[
+            jax.ShapeDtypeStruct((count, batches, tokens, part), BF),
+            jax.ShapeDtypeStruct(weight.shape, BF),
+        ],
+        in_specs=[anywhere] * 3,
+        out_specs=[anywhere] * 2,
+        scratch_shapes=[dma((count - 1,)), dma((count - 1,)), dma, dma, dma],
+        compiler_params=pltpu.CompilerParams(collective_id=collective_id, has_side_effects=True),
+        cost_estimate=pl.CostEstimate(
+            flops=inputs.size, bytes_accessed=inputs.size * 40, transcendentals=0
+        ),
+        name="spread",
+    )(inputs, cotangent, weight)
+
+
 def mm(a, b, ca, cb):
     return lax.dot_general(a, b, (((ca,), (cb,)), ((), ())), preferred_element_type=F32)
 
@@ -368,10 +437,7 @@
     a_own = w_in[0]
     b_own = w_out[0].T
     hidden = a_own.shape[1]
-    v_other = swap_pipe(jnp.where(first, b_own, a_own))
-    mine = lax.all_to_all(
-        jnp.where(first, inputs, cotangent), "dp", split_axis=2, concat_axis=1, tiled=True
-    )
+    mine, v_other = spread(inputs, cotangent, jnp.where(first, b_own, a_own), 4)
     mine = mine.reshape(-1, mine.shape[-1])
     v_own = jnp.where(first, a_own, b_own)
 

time: 278 us -> 244 us (0.88)
  waiting for transfers between devices: 45.4 us -> 0.01 us
  Pallas kernels: 144 us -> 188 us
  local copies, waits for them, and re-layouts: 23 us -> 4.67 us
  starting transfers between devices: 11.6 us -> 1.85 us
  matrix products: 31.9 us -> 29 us
    pallas_call x0 -> x1, Pallas kernels: none -> 52.3 us  [spread(): pl.pallas_call(kernel, out_shape=[jax.ShapeDtypeStruct((count, batches, t...]
    ppermute x3 -> x2, waiting for transfers between devices: 45.4 us -> 0.01 us  [swap_pipe(): return lax.ppermute(value, 'pipe', [(0, 1), (1, 0)])]
    unnamed x17, local copies, waits for them, and re-layouts: 15.1 us -> 2.9 us
    all_to_all x1 -> x0, starting transfers between devices: 6.35 us -> none  [on_device(): lax.all_to_all(jnp.where(first, inputs, cotangent), 'dp', split_axis=2, c...]
    all_to_all x1 -> x0, local copies, waits for them, and re-layouts: 6.16 us -> none  [on_device(): lax.all_to_all(jnp.where(first, inputs, cotangent), 'dp', split_axis=2, c...]
    pallas_call x1, Pallas kernels: 50.8 us -> 47 us  [reduce_rows(): pl.pallas_call(kernel, out_shape=[jax.ShapeDtypeStruct((shape[0] // ways,...]
    ppermute x3 -> x2, starting transfers between devices: 5.3 us -> 1.85 us  [swap_pipe(): return lax.ppermute(value, 'pipe', [(0, 1), (1, 0)])]
    dot_general x8, matrix products: 31.9 us -> 29 us  [mm(): lax.dot_general(a, b, (((ca,), (cb,)), ((), ())), preferred_element_type=...]
  transfers between devices with their start and end apart: 4 -> 2, of which waited for: 1 -> 0; matrix products, arithmetic and copies ran while one was open for 7% -> 8% of each run, Pallas kernels for 47% -> 51%
where the time goes in v3:
time: 244 us
  Pallas kernels  188 us (77%)
  matrix products  29 us (12%)
  other arithmetic  16.4 us (7%)
  local copies, waits for them, and re-layouts  4.67 us (2%)
  between operations  4.01 us (2%)
    pallas_call x2, Pallas kernels, gather_rows(): pl.pallas_call(kernel, out_shape=jax.ShapeDtypeStruct((rows_all, width),...  77.2 us
    pallas_call x1, Pallas kernels, spread(): pl.pallas_call(kernel, out_shape=[jax.ShapeDtypeStruct((count, batches, t...  52.3 us
    pallas_call x1, Pallas kernels, reduce_rows(): pl.pallas_call(kernel, out_shape=[jax.ShapeDtypeStruct((shape[0] // ways,...  47 us
    dot_general x8, matrix products, mm(): lax.dot_general(a, b, (((ca,), (cb,)), ((), ())), preferred_element_type=...  29 us
    pallas_call x1, Pallas kernels, sum_all(): pl.pallas_call(kernel, out_shape=jax.ShapeDtypeStruct((8, 128), F32), in_...  11.3 us
    broadcast_in_dim x1, other arithmetic, on_device(): return ((total_in * factor)[None], (total_out * factor)[None], grad_norm)  8.78 us
  transfers between devices with their start and end apart: 2, of which 0 were waited for; matrix products, arithmetic and copies ran while one was open for 8% of the time, Pallas kernels for 51%

profile of v3, /device:TPU:0, one launch (start us, length us, event | category | flops | bytes accessed | tf_op | source)
XLA Modules:
  0.0 243.8 jit_solution(15634556107926355566)
XLA Ops:
  0.6 2.9 %copy.7 = bf16[1,1024,1024]{1,2,0:T(8,128)(2,1)S(1)} copy(bf16[1,1024,1024]{2,1,0:T(8,128)(2,1)} %param.6) | data formatting | bytes 4194304 | tf_op args[2]
  3.5 3.1 %bitcast_select_fusion.2.w_ref = bf16[1024,1024]{1,0:T(8,128)(2,1)} fusion(bf16[1,1024,1024]{1,2,0:T(8,128)(2,1)S(1)} %copy.7, bf16[1,1024,1024]{2,1,0:T(8,128)(2,1)} %param.5, pred[]{:T(512)S(6)} %eq.3), kind=kLoop, calls=%fused_computation.8 | loop fusion | flops 1048576 | bytes 6291457 | tf_op jit(solution)/shard_map/jit(_where)/select_n | solution.py:440
  6.6 52.3 %spread.1 = (bf16[4,2,128,1024]{3,2,1,0:T(8,128)(2,1)}, bf16[1024,1024]{1,0:T(8,128)(2,1)}) custom-call(bf16[2,128,4096]{2,1,0:T(8,128)(2,1)} %in_ref.1, bf16[2,128,4096]{2,1,0:T(8,128)(2,1)} %cot_ref.1, bf16[1024,1024]{1,0:T(8,128)(2,1)} %bitcast_select_fusion.2.w_ref), custom_call_target="tpu_custom_call" | custom-call | flops 1048576 | bytes 41943040 | tf_op jit(solution)/shard_map/spread/pallas_call | solution.py:398
  59.0 0.0 copy-start.1
  59.0 0.6 collective-permute-start
  59.6 4.9 %fusion.15 = bf16[1024,1024]{1,0:T(8,128)(2,1)S(1)} fusion(bf16[1024,1024]{1,0:T(8,128)(2,1)} %bitcast.38, bf16[1,1024,1024]{1,2,0:T(8,128)(2,1)S(1)} %copy.7, bf16[1,1024,1024]{2,1,0:T(8,128)(2,1)} %param.5, pred[]{:T(512)S(6)} %eq.3), kind=kOutput, calls=%fused_computation.25 | convolution fusion | flops 2149580800 | bytes 8388609 | tf_op jit(solution)/shard_map/dot_general | solution.py:416
  64.4 0.0 copy-done.1
  64.5 0.0 copy-done.6
  64.5 0.0 copy-start.4
  64.5 3.8 %fusion.16.refs_0_ = bf16[1024,1024]{1,0:T(8,128)(2,1)} fusion(bf16[1024,1024]{1,0:T(8,128)(2,1)S(1)} %copy-done.6, bf16[1,1024,1024]{2,1,0:T(8,128)(2,1)S(1)} %copy-done.1, pred[]{:T(512)S(6)} %eq.3, bf16[1,1024,1024]{1,2,0:T(8,128)(2,1)S(1)} %copy.7), kind=kOutput, calls=%fused_computation.26 | convolution fusion | flops 2150629376 | bytes 8388609 | tf_op jit(solution)/shard_map/dot_general | solution.py:416
  68.3 2.3 convolution_convert_fusion
  70.6 2.5 %pad_maximum_fusion.refs_1_ = bf16[1024,2048]{1,0:T(8,128)(2,1)} fusion(bf16[1024,1024]{1,0:T(8,128)(2,1)S(1)} %convolution_convert_fusion, bf16[1024,1024]{1,0:T(8,128)(2,1)S(1)} %fusion.15), kind=kLoop, calls=%fused_computation | loop fusion | flops 8388608 | bytes 8388608 | tf_op jit(solution)/shard_map/concatenate | solution.py:448
  73.1 47.0 %reduce_rows.1 = (bf16[64,1024]{1,0:T(8,128)(2,1)}, f32[64,2048]{1,0:T(8,128)}) custom-call(bf16[1024,1024]{1,0:T(8,128)(2,1)} %fusion.16.refs_0_, bf16[1024,2048]{1,0:T(8,128)(2,1)} %pad_maximum_fusion.refs_1_), custom_call_target="tpu_custom_call" | custom-call | flops 3145728 | bytes 125829120 | tf_op jit(solution)/shard_map/reduce_rows/pallas_call | solution.py:178
  120.1 0.0 copy-start.3
  120.1 1.1 convert_element_type.30
  121.2 1.3 collective-permute-start.1
  122.5 23.0 %gather_rows.2 = bf16[1024,1024]{1,0:T(8,128)(2,1)} custom-call(bf16[64,1024]{1,0:T(8,128)(2,1)} %get-tuple-element.10.in_ref), custom_call_target="tpu_custom_call" | custom-call | flops 1048576 | bytes 41943040 | tf_op jit(solution)/shard_map/gather_rows/pallas_call | solution.py:272
  145.6 0.0 collective-permute-done.1
  145.6 0.1 convert_select_fusion.1
  145.7 0.0 copy-start.2
  145.7 2.3 broadcast_select_fusion.1
  148.0 0.8 broadcast_select_fusion
  148.8 0.8 pad_maximum_fusion.1.in_ref
  149.6 54.2 %gather_rows.3 = bf16[1024,3072]{1,0:T(8,128)(2,1)} custom-call(bf16[64,3072]{1,0:T(8,128)(2,1)} %pad_maximum_fusion.1.in_ref), custom_call_target="tpu_custom_call" | custom-call | flops 3145728 | bytes 125829120 | tf_op jit(solution)/shard_map/gather_rows/pallas_call | solution.py:272
  203.8 0.0 collective-permute-done
  203.9 4.7 %add_convert_fusion = bf16[1024,1024]{1,0:T(8,128)(2,1)S(1)} fusion(bf16[1024,1024]{1,0:T(8,128)(2,1)} %collective-permute-done, bf16[1024,1024]{1,0:T(8,128)(2,1)S(1)} %copy-done.7, bf16[1024,3072]{1,0:T(8,128)(2,1)} %gather_rows.3), kind=kOutput, calls=%fused_computation.5 | convolution fusion | flops 2150629376 | bytes 8388608 | tf_op jit(solution)/shard_map/dot_general | solution.py:416
  208.6 5.0 %multiply_reduce_fusion = (f32[]{:T(128)}, f32[1024,1024]{1,0:T(8,128)}) fusion(bf16[1024,1024]{1,0:T(8,128)(2,1)S(1)} %add_convert_fusion, bf16[1024,1024]{1,0:T(8,128)(2,1)S(1)} %bitcast.40, pred[]{:T(512)S(6)} %eq.3, bf16[1024,3072]{1,0:T(8,128)(2,1)S(1)} %copy-done), kind=kOutput, calls=%fused_computation.3 | convolution fusion | flops 2150629376 | bytes 10485765 | tf_op jit(solution)/shard_map/dot_general | solution.py:416
  213.6 5.2 %multiply_reduce_fusion.1 = (f32[]{:T(128)}, f32[1024,1024]{1,0:T(8,128)}) fusion(bf16[1024,3072]{1,0:T(8,128)(2,1)S(1)} %copy-done, bf16[1024,1024]{1,0:T(8,128)(2,1)S(1)} %bitcast.41, bf16[1024,1024]{1,0:T(8,128)(2,1)S(1)} %add_convert_fusion, pred[]{:T(512)S(6)} %eq.3), kind=kOutput, calls=%fused_computation.4 | convolution fusion | flops 2150629376 | bytes 10485765 | tf_op jit(solution)/shard_map/dot_general | solution.py:416
  220.1 0.6 broadcast_in_dim.9.in_ref
  220.7 11.3 %sum_all.1 = f32[8,128]{1,0:T(8,128)} custom-call(f32[8,128]{1,0:T(8,128)} %broadcast_in_dim.9.in_ref), custom_call_target="tpu_custom_call" | custom-call | tf_op jit(solution)/shard_map/sum_all/pallas_call | solution.py:335
  231.9 1.2 slice.31
  233.9 8.8 %multiply_bitcast_fusion = (f32[1,1024,1024]{2,1,0:T(8,128)}, f32[1,1024,1024]{2,1,0:T(8,128)}) fusion(f32[1024,1024]{1,0:T(8,128)} %get-tuple-element.19, f32[]{:T(128)S(6)} %min.3, f32[1024,1024]{1,0:T(8,128)} %get-tuple-element.17), kind=kLoop, calls=%fused_computation.1 | loop fusion | flops 2097152 | bytes 16777220 | tf_op jit(solution)/shard_map/broadcast_in_dim | solution.py:476
  (10 shorter events, 0.0 us)
Async XLA Ops:
  59.0 5.5 %copy-start.1 = (bf16[1,1024,1024]{2,1,0:T(8,128)(2,1)S(1)}, bf16[1,1024,1024]{2,1,0:T(8,128)(2,1)}, u32[]{:S(2)}) copy-start(bf16[1,1024,1024]{2,1,0:T(8,128)(2,1)} %param.5) | copy-start | bytes 6291460
  59.0 5.5 %copy-start.6 = (bf16[1024,1024]{1,0:T(8,128)(2,1)S(1)}, bf16[1024,1024]{1,0:T(8,128)(2,1)}, u32[]{:S(2)}) copy-start(bf16[1024,1024]{1,0:T(8,128)(2,1)} %get-tuple-element.8) | copy-start | bytes 6291460
  59.0 144.9 %collective-permute-start = (bf16[1024,1024]{1,0:T(8,128)(2,1)}, bf16[1024,1024]{1,0:T(8,128)(2,1)}, u32[]{:S(2)}, u32[]{:S(2)}) collective-permute-start(bf16[1024,1024]{1,0:T(8,128)(2,1)} %bitcast.37), channel_id=1, source_target_pairs={{0,16},{16,0},{1,17},{17,1},{2,18},{18,2},{3,19},{19,3},{4,20},{20... | collective-permute-start | bytes 6291464 | tf_op jit(solution)/shard_map/ppermute | solution.py:420
  64.5 3.8 %copy-start.4 = (bf16[4,2,128,1024]{3,2,1,0:T(8,128)(2,1)S(1)}, bf16[4,2,128,1024]{3,2,1,0:T(8,128)(2,1)}, u32[]{:S(2)}) copy-start(bf16[4,2,128,1024]{3,2,1,0:T(8,128)(2,1)} %get-tuple-element.7) | copy-start | bytes 6291460
  120.1 25.5 %copy-start.3 = (f32[64,2048]{1,0:T(8,128)S(1)}, f32[64,2048]{1,0:T(8,128)}, u32[]{:S(2)}) copy-start(f32[64,2048]{1,0:T(8,128)} %get-tuple-element.9) | copy-start | bytes 1572868
  121.2 24.3 %collective-permute-start.1 = (bf16[64,2048]{1,0:T(8,128)(2,1)S(1)}, bf16[64,2048]{1,0:T(8,128)(2,1)S(1)}, u32[]{:S(2)}, u32[]{:S(2)}) collective-permute-start(bf16[64,2048]{1,0:T(8,128)(2,1)S(1)} %convert_element_type.30), channel_id=1, source_target_pairs={{0,16},{16,0},{1,17},{17,1},{2,18},{18,2},{3,19},{19,3},{4,20},{20... | collective-permute-start | bytes 786440 | tf_op jit(solution)/shard_map/ppermute | solution.py:420
  145.7 2.3 copy-start.2
  149.6 54.2 %copy-start.7 = (bf16[1024,1024]{1,0:T(8,128)(2,1)S(1)}, bf16[1024,1024]{1,0:T(8,128)(2,1)}, u32[]{:S(2)}) copy-start(bf16[1024,1024]{1,0:T(8,128)(2,1)} %get-tuple-element.8) | copy-start | bytes 6291460
  203.8 4.8 %copy-start = (bf16[1024,3072]{1,0:T(8,128)(2,1)S(1)}, bf16[1024,3072]{1,0:T(8,128)(2,1)}, u32[]{:S(2)}) copy-start(bf16[1024,3072]{1,0:T(8,128)(2,1)} %gather_rows.3) | copy-start | bytes 18874372
  203.8 4.8 %copy-start.5 = (bf16[4,2,128,1024]{3,2,1,0:T(8,128)(2,1)S(1)}, bf16[4,2,128,1024]{3,2,1,0:T(8,128)(2,1)}, u32[]{:S(2)}) copy-start(bf16[4,2,128,1024]{3,2,1,0:T(8,128)(2,1)} %get-tuple-element.7) | copy-start | bytes 6291460
